TPU v7x, 256 devices: a 2x2x32 block of a 4x8x32 slice. The times are simulated.
256 devices in a mesh: groups: 4 (over x, y), feat: 64 (over z, core).
Axes of the slice: x: 2, y: 2, z: 32, core: 2. Of those that a mesh axis runs over, the one named last changes fastest.
The devices are a block of a 4x8x32 slice.
Arguments:
- cells: bfloat16 [768, 512, 192], P('groups', 'feat'), parts along dimension 0, may hold values from -6 to 6
- missing: int32 [768, 512], P('groups', 'feat'), parts along dimension 0, may hold values 0 or 1
- feat_ids: int32 [2048], P(('groups', 'feat')), parts along dimension 0, may hold values from 0 to 63
- feat_table: float32 [64, 192], replicated, may hold values from -5 to 5
- nan_embed: float32 [192], replicated, may hold values from -5 to 5
- gain_one: float32 [192], replicated, may hold values from 0.1 to 1.9
- w_qkv: bfloat16 [192, 576], replicated, may hold values from -3 to 3
- w_out: bfloat16 [192, 192], replicated, may hold values from -0.4375 to 0.4375
- gain_two: float32 [192], replicated, may hold values from 0.1 to 1.9
- w_up: bfloat16 [192, 768], replicated, may hold values from -0.4375 to 0.4375
- w_down: bfloat16 [768, 192], replicated, may hold values from -0.21875 to 0.21875
Outputs:
- result: float32 [768, 512, 192], P('groups', 'feat'), parts along dimension 0
There are 4 independent parts, one for each index of `groups`. A program takes and returns all parts, laid end to end along the dimension named above; an argument that names none is the same for every part. Nothing has to cross between parts.
All inputs are finite; a program needn't handle non-finite values. No bound on the sum of `missing` on one device may be relied on, other than what follows from the above.
Results may differ from a plain program's by a relative error of at most 0.007.
The roundings to bfloat16 on the way count: a program that leaves them out, or rounds other values in their place, can miss the bound.
Values may be sent and summed in bfloat16 or wider, within the bound.
No kernel may reach another device: no remote copies, remote signals or barrier semaphores. Data moves between devices by JAX's collectives and lax.ppermute only.
A program may use at most 64 MiB of HBM per device.

v0:
```python
import jax
import jax.numpy as jnp
from jax import lax
from jax.sharding import Mesh
from jax.sharding import PartitionSpec as P

HEADS = 6
FEAT = ("feat_0", "feat_1")
GROUPS_FEAT = ("groups", "feat_0", "feat_1")


def split_up(x, dim, devices):
    before, after = (x.shape[:dim], x.shape[dim + 1 :])
    return jnp.moveaxis(x.reshape(*before, devices, -1, *after), dim, 0)


def joined_along(tiles, dim):
    tiles = jnp.moveaxis(tiles, 0, dim)
    lengths = tiles.shape
    return tiles.reshape(*lengths[:dim], lengths[dim] * lengths[dim + 1], *lengths[dim + 2 :])


def moved_by_axis(tiles, axes, sequence):
    inside = tiles.shape[1:]
    filled = tiles.reshape(*(lax.axis_size(a) for a in axes), *inside)
    for k in sequence:
        filled = lax.all_to_all(filled, axes[k], k, k, tiled=True)
    return filled.reshape(-1, *inside)


def core_and_chips(x, groups, sequence, split_dim, concat_dim):
    devices = lax.axis_size(groups[0]) * lax.axis_size(groups[1])
    tiles = split_up(x, split_dim, devices)
    return joined_along(moved_by_axis(tiles, groups, sequence), concat_dim)


def cell_norm(values, gain):
    mean = jnp.mean(values, axis=-1, keepdims=True)
    centered = values - mean
    var = jnp.mean(centered * centered, axis=-1, keepdims=True)
    return centered * lax.rsqrt(var + 1e-05) * gain


def attend(qkv):
    width = qkv.shape[-1] // 3
    count = qkv.shape[0]
    head_dim = width // HEADS
    query = qkv[:, :width].reshape(count, HEADS, head_dim)
    keys = qkv[:, width : 2 * width].reshape(count, HEADS, head_dim)
    values = qkv[:, 2 * width :].reshape(count, HEADS, head_dim)
    scores = jnp.einsum(
        "qhd,phd->hqp", query, keys, preferred_element_type=jnp.float32
    ) * head_dim ** (-0.5)
    top = jnp.max(scores, axis=-1, keepdims=True)
    expo = jnp.exp(scores - top)
    probs = (expo / jnp.sum(expo, axis=-1, keepdims=True)).astype(jnp.bfloat16)
    context = jnp.einsum("hqp,phd->qhd", probs, values, preferred_element_type=jnp.float32)
    return context.astype(jnp.bfloat16).reshape(count, width)


def finish(base, context, w_out, gain_two, w_up, w_down):
    mid = base + jnp.dot(context, w_out, preferred_element_type=jnp.float32)
    normed_two = cell_norm(mid, gain_two).astype(jnp.bfloat16)
    act = jax.nn.gelu(
        jnp.dot(normed_two, w_up, preferred_element_type=jnp.float32), approximate=False
    ).astype(jnp.bfloat16)
    return mid + jnp.dot(act, w_down, preferred_element_type=jnp.float32)


def body(
    cells, missing, feat_ids, feat_table, nan_embed, gain_one, w_qkv, w_out, gain_two, w_up, w_down
):
    devices = lax.axis_size(FEAT)
    all_rows, local_feats, width = cells.shape
    onehot = (
        feat_ids[:, None] == jnp.arange(feat_table.shape[0], dtype=jnp.int32)[None, :]
    ).astype(jnp.float32)
    femb = jnp.dot(onehot, feat_table, precision=lax.Precision.HIGHEST)
    tokens = (
        cells.astype(jnp.float32) + missing[..., None].astype(jnp.float32) * nan_embed + femb[None]
    ).astype(jnp.bfloat16)

    def one_row(row):
        base = row.astype(jnp.float32)
        normed = cell_norm(base, gain_one).astype(jnp.bfloat16)
        qkv = jnp.dot(normed, w_qkv, preferred_element_type=jnp.float32).astype(jnp.bfloat16)
        return finish(base, attend(qkv), w_out, gain_two, w_up, w_down)

    grouped = tokens.reshape(devices, all_rows // devices, local_feats, width)
    outputs = lax.map(one_row, core_and_chips(grouped, ("feat_0", "feat_1"), (1, 0), 0, 2)[0])
    back = core_and_chips(
        outputs[None].astype(jnp.bfloat16), ("feat_0", "feat_1"), (1, 0), 2, 0
    ).astype(jnp.float32)
    return back.reshape(all_rows, local_feats, width)


def solution(mesh):
    split = Mesh(mesh.devices.reshape(mesh.shape["groups"], 32, 2), ("groups", "feat_0", "feat_1"))
    in_specs = (
        P("groups", FEAT, None),
        P("groups", FEAT),
        P(GROUPS_FEAT),
        P(),
        P(),
        P(),
        P(),
        P(),
        P(),
        P(),
        P(),
    )
    out_specs = P("groups", FEAT, None)
    return jax.shard_map(body, mesh=split, in_specs=in_specs, out_specs=out_specs, check_vma=False)
```

profile of v0, /device:TPU:37, one launch (start us, length us, event | category | flops | bytes accessed | tf_op | source)
XLA Modules:
  0.0 264.8 jit_solution(11658586414275395537)
XLA Ops:
  0.0 0.0 copy-start
  0.0 0.7 convert_element_type.50
  0.7 0.1 copy.31
  0.8 0.0 copy-done
  0.9 0.8 fusion.102
  1.7 1.5 add_convert_fusion
  3.2 0.1 copy.32
  3.3 24.4 %all_to_all.20 = bf16[32,2,1,3,8,192]{5,4,3,0,2,1:T(8,128)(2,1)S(1)} all-to-all(bf16[32,2,1,3,8,192]{5,4,3,0,2,1:T(8,128)(2,1)S(1)} %copy.32), channel_id=1, replica_groups=mesh['groups'=4,'feat_0'=32,'feat_1'=2] {'feat_1'}, dimensions={1} | all-to-all | bytes 1179648 | tf_op jit(solution)/shard_map/all_to_all | solution.py:27
  27.7 0.9 copy.33
  28.6 13.4 %all-to-all-start.1 = ((bf16[32,2,1,3,8,192]{5,4,3,1,2,0:T(8,128)(2,1)}), bf16[32,2,1,3,8,192]{5,4,3,1,2,0:T(8,128)(2,1)S(1)}, u32[]{:S(2)}, u32[]{:S(2)}) async-start(bf16[32,2,1,3,8,192]{5,4,3,1,2,0:T(8,128)(2,1)} %copy.33), calls=%async_computation.1 | async-start | bytes 1572864 | tf_op jit(solution)/shard_map/all_to_all | solution.py:27
  42.0 0.0 copy-start.1
  42.0 0.0 copy-start.2
  42.0 0.0 copy-start.3
  42.0 0.0 copy-start.4
  42.1 0.0 copy-start.5
  42.1 0.0 copy-start.6
  42.1 85.7 %all-to-all-done.1 = bf16[32,2,1,3,8,192]{5,4,3,1,2,0:T(8,128)(2,1)S(1)} async-done(((bf16[32,2,1,3,8,192]{5,4,3,1,2,0:T(8,128)(2,1)}), bf16[32,2,1,3,8,192]{5,4,3,1,2,0:T(8,128)(2,1)S(1)}, u32[]{:S(2)}, u32[]{:S(2)}) %all-to-all-start.1) | async-done | bytes 589856 | tf_op jit(solution)/shard_map/all_to_all | solution.py:27
  127.8 0.1 copy.42
  127.8 0.3 copy.35
  128.1 0.0 copy-done.1
  128.1 0.0 copy-done.2
  128.1 0.0 copy-done.3
  128.1 0.0 copy-done.4
  128.1 0.0 copy-done.5
  128.1 0.0 copy-done.6
  128.1 39.8 %while.10 = (s32[]{:T(128)}, bf16[3,512,192]{1,2,0:T(8,128)(2,1)S(1)}, bf16[3,512,192]{1,2,0:T(8,128)(2,1)S(1)}, f32[192]{0:T(256)S(1)}, bf16[192,576]{1,0:T(8,1...) while((s32[]{:T(128)}, ...), condition=%wide.region_7.8_spmd, body=%wide.region_0.7_spmd.sunk | while | flops 690292224 | bytes 19060856 | solution.py:90
  128.2 0.1 convert_reduce_fusion.2
  128.2 0.1 fusion.142
  128.3 0.4 convolution_convert_fusion.2
  128.8 4.8 %fusion.144 = (f32[6,512]{1,0:T(8,128)S(1)}, f32[6,512,512]{1,2,0:T(8,128)}) fusion(bf16[512,6,32]{0,2,1:T(8,128)(2,1)S(1)} %bitcast.85, bf16[512,6,32]{0,2,1:T(8,128)(2,1)S(1)} %bitcast.84), kind=kOutput, calls=%fused_computation.124.clone.1 | convolution fusion | flops 105382400 | bytes 6696960 | tf_op jit(solution)/shard_map/while/body/eval_jaxpr/sub | solution.py:55
  133.6 3.4 %fusion.145 = bf16[6,32,512]{2,1,0:T(8,128)(2,1)S(1)} fusion(bf16[512,6,32]{0,2,1:T(8,128)(2,1)S(1)} %bitcast.83, f32[6,512,512]{1,2,0:T(8,128)} %get-tuple-element.170, f32[6,512]{1,0:T(8,128)S(1)} %get-tuple-element.171), kind=kOutput, calls=%fused_computation.32.clone.1 | convolution fusion | flops 103907328 | bytes 6696960 | tf_op jit(solution)/shard_map/while/body/eval_jaxpr/hqp,phd->qhd/dot_general | solution.py:57
  137.0 0.3 fusion.146
  137.3 0.1 multiply_reduce_fusion.3
  137.4 4.1 %fusion.147 = bf16[3,512,192]{1,2,0:T(8,128)(2,1)S(1)} fusion(bf16[3,512,192]{1,2,0:T(8,128)(2,1)S(1)} %get-tuple-element.185, s32[]{:T(128)} %get-tuple-element.184, f32[512,192]{0,1:T(8,128)S(1)} %get-tuple-element.172, bf16[768,192]{0,1:T(8,128)(2,1)S(1)} %get-tuple-element.202, bf16[192,768]{1,0:T(8,128)(2,1)S(1)} %get-tuple-element.201, ...), kind=kOutput, calls=%fused_computation.31.clone.1 | convolution fusion | flops 328040448 | bytes 1774596 | tf_op jit(solution)/shard_map/while/body/eval_jaxpr/dot_general | solution.py:67
  141.4 0.1 convert_reduce_fusion.2
  141.5 0.1 fusion.142
  141.6 0.4 convolution_convert_fusion.2
  142.1 4.8 %fusion.144 = (f32[6,512]{1,0:T(8,128)S(1)}, f32[6,512,512]{1,2,0:T(8,128)}) fusion(bf16[512,6,32]{0,2,1:T(8,128)(2,1)S(1)} %bitcast.85, bf16[512,6,32]{0,2,1:T(8,128)(2,1)S(1)} %bitcast.84), kind=kOutput, calls=%fused_computation.124.clone.1 | convolution fusion | flops 105382400 | bytes 6696960 | tf_op jit(solution)/shard_map/while/body/eval_jaxpr/sub | solution.py:55
  146.8 3.4 %fusion.145 = bf16[6,32,512]{2,1,0:T(8,128)(2,1)S(1)} fusion(bf16[512,6,32]{0,2,1:T(8,128)(2,1)S(1)} %bitcast.83, f32[6,512,512]{1,2,0:T(8,128)} %get-tuple-element.170, f32[6,512]{1,0:T(8,128)S(1)} %get-tuple-element.171), kind=kOutput, calls=%fused_computation.32.clone.1 | convolution fusion | flops 103907328 | bytes 6696960 | tf_op jit(solution)/shard_map/while/body/eval_jaxpr/hqp,phd->qhd/dot_general | solution.py:57
  150.3 0.3 fusion.146
  150.6 0.1 multiply_reduce_fusion.3
  150.6 4.1 %fusion.147 = bf16[3,512,192]{1,2,0:T(8,128)(2,1)S(1)} fusion(bf16[3,512,192]{1,2,0:T(8,128)(2,1)S(1)} %get-tuple-element.185, s32[]{:T(128)} %get-tuple-element.184, f32[512,192]{0,1:T(8,128)S(1)} %get-tuple-element.172, bf16[768,192]{0,1:T(8,128)(2,1)S(1)} %get-tuple-element.202, bf16[192,768]{1,0:T(8,128)(2,1)S(1)} %get-tuple-element.201, ...), kind=kOutput, calls=%fused_computation.31.clone.1 | convolution fusion | flops 328040448 | bytes 1774596 | tf_op jit(solution)/shard_map/while/body/eval_jaxpr/dot_general | solution.py:67
  154.7 0.1 convert_reduce_fusion.2
  154.8 0.1 fusion.142
  154.9 0.4 convolution_convert_fusion.2
  155.3 4.8 %fusion.144 = (f32[6,512]{1,0:T(8,128)S(1)}, f32[6,512,512]{1,2,0:T(8,128)}) fusion(bf16[512,6,32]{0,2,1:T(8,128)(2,1)S(1)} %bitcast.85, bf16[512,6,32]{0,2,1:T(8,128)(2,1)S(1)} %bitcast.84), kind=kOutput, calls=%fused_computation.124.clone.1 | convolution fusion | flops 105382400 | bytes 6696960 | tf_op jit(solution)/shard_map/while/body/eval_jaxpr/sub | solution.py:55
  160.1 3.4 %fusion.145 = bf16[6,32,512]{2,1,0:T(8,128)(2,1)S(1)} fusion(bf16[512,6,32]{0,2,1:T(8,128)(2,1)S(1)} %bitcast.83, f32[6,512,512]{1,2,0:T(8,128)} %get-tuple-element.170, f32[6,512]{1,0:T(8,128)S(1)} %get-tuple-element.171), kind=kOutput, calls=%fused_computation.32.clone.1 | convolution fusion | flops 103907328 | bytes 6696960 | tf_op jit(solution)/shard_map/while/body/eval_jaxpr/hqp,phd->qhd/dot_general | solution.py:57
  163.5 0.3 fusion.146
  163.8 0.1 multiply_reduce_fusion.3
  163.9 4.1 %fusion.147 = bf16[3,512,192]{1,2,0:T(8,128)(2,1)S(1)} fusion(bf16[3,512,192]{1,2,0:T(8,128)(2,1)S(1)} %get-tuple-element.185, s32[]{:T(128)} %get-tuple-element.184, f32[512,192]{0,1:T(8,128)S(1)} %get-tuple-element.172, bf16[768,192]{0,1:T(8,128)(2,1)S(1)} %get-tuple-element.202, bf16[192,768]{1,0:T(8,128)(2,1)S(1)} %get-tuple-element.201, ...), kind=kOutput, calls=%fused_computation.31.clone.1 | convolution fusion | flops 328040448 | bytes 1774596 | tf_op jit(solution)/shard_map/while/body/eval_jaxpr/dot_general | solution.py:67
  168.0 0.3 copy.36
  168.2 0.1 copy.37
  168.3 5.6 %all_to_all.21 = bf16[32,2,1,3,8,192]{5,4,0,3,2,1:T(8,128)(2,1)S(1)} all-to-all(bf16[32,2,1,3,8,192]{5,4,0,3,2,1:T(8,128)(2,1)S(1)} %copy.37), channel_id=1, replica_groups=mesh['groups'=4,'feat_0'=32,'feat_1'=2] {'feat_1'}, dimensions={1} | all-to-all | bytes 1179648 | tf_op jit(solution)/shard_map/all_to_all | solution.py:27
  173.9 0.1 copy.38
  174.0 89.4 %all_to_all.22 = bf16[32,2,1,3,8,192]{5,4,1,3,2,0:T(8,128)(2,1)S(1)} all-to-all(bf16[32,2,1,3,8,192]{5,4,1,3,2,0:T(8,128)(2,1)S(1)} %copy.38), channel_id=1, replica_groups=mesh['groups'=4,'feat_0'=32,'feat_1'=2] {'feat_0'}, dimensions={0} | all-to-all | bytes 1179648 | tf_op jit(solution)/shard_map/all_to_all | solution.py:27
  263.4 0.1 copy.39
  263.5 1.3 bitcast_convert_fusion
  (16 shorter events, 0.2 us)
Async XLA Ops:
  0.0 0.8 copy-start
  28.6 99.2 %all-to-all-start.1 = ((bf16[32,2,1,3,8,192]{5,4,3,1,2,0:T(8,128)(2,1)}), bf16[32,2,1,3,8,192]{5,4,3,1,2,0:T(8,128)(2,1)S(1)}, u32[]{:S(2)}, u32[]{:S(2)}) async-start(bf16[32,2,1,3,8,192]{5,4,3,1,2,0:T(8,128)(2,1)} %copy.33), calls=%async_computation.1 | async-start | bytes 1572864 | tf_op jit(solution)/shard_map/all_to_all | solution.py:27
  42.0 86.1 %copy-start.1 = (bf16[192,576]{1,0:T(8,128)(2,1)S(1)}, bf16[192,576]{1,0:T(8,128)(2,1)}, u32[]{:S(2)}) copy-start(bf16[192,576]{1,0:T(8,128)(2,1)} %param.19) | copy-start | bytes 663556
  42.0 86.1 %copy-start.2 = (bf16[192,192]{1,0:T(8,128)(2,1)S(1)}, bf16[192,192]{1,0:T(8,128)(2,1)}, u32[]{:S(2)}) copy-start(bf16[192,192]{1,0:T(8,128)(2,1)} %param.20) | copy-start | bytes 221188
  42.0 86.1 %copy-start.3 = (f32[192]{0:T(256)S(1)}, f32[192]{0:T(256)}, u32[]{:S(2)}) copy-start(f32[192]{0:T(256)} %param.18) | copy-start | bytes 2308
  42.0 86.1 %copy-start.4 = (bf16[192,768]{1,0:T(8,128)(2,1)S(1)}, bf16[192,768]{1,0:T(8,128)(2,1)}, u32[]{:S(2)}) copy-start(bf16[192,768]{1,0:T(8,128)(2,1)} %param.22) | copy-start | bytes 884740
  42.1 86.1 %copy-start.5 = (bf16[768,192]{0,1:T(8,128)(2,1)S(1)}, bf16[768,192]{0,1:T(8,128)(2,1)}, u32[]{:S(2)}) copy-start(bf16[768,192]{0,1:T(8,128)(2,1)} %param.23) | copy-start | bytes 884740
  42.1 86.1 %copy-start.6 = (f32[192]{0:T(256)S(1)}, f32[192]{0:T(256)}, u32[]{:S(2)}) copy-start(f32[192]{0:T(256)} %param.21) | copy-start | bytes 2308
where the time goes:
time: 266 us; the launch traced here: 265 us
  blocking collectives  119 us (45%)
  waiting for transfers between devices  85.7 us (32%)
  matrix products  39.7 us (15%)
  starting transfers between devices  13.4 us (5%)
  other arithmetic  4.23 us (2%)
    all_to_all x3, blocking collectives, moved_by_axis(): filled = lax.all_to_all(filled, axes[k], k, k, tiled=True)  119 us
    all_to_all x1, waiting for transfers between devices, moved_by_axis(): filled = lax.all_to_all(filled, axes[k], k, k, tiled=True)  85.7 us
    sub x3, matrix products, attend(): expo = jnp.exp(scores - top)  14.3 us
    all_to_all x1, starting transfers between devices, moved_by_axis(): filled = lax.all_to_all(filled, axes[k], k, k, tiled=True)  13.4 us
    dot_general x3, matrix products, finish(): return mid + jnp.dot(act, w_down, preferred_element_type=jnp.float32)  12.2 us
    dot_general x3, matrix products, attend(): jnp.einsum('hqp,phd->qhd', probs, values, preferred_element_type=jnp.floa...  10.3 us
  transfers between devices with their start and end apart: 1, of which 1 were waited for; matrix products, arithmetic and copies ran while one was open for 0% of the time, Pallas kernels for 0%

commit v1 on v0

v1 whole, which is shorter than its diff:
```python
import functools

import jax
import jax.numpy as jnp
from jax import lax
from jax.experimental import pallas as pl
from jax.experimental.pallas import tpu as pltpu
from jax.sharding import Mesh
from jax.sharding import PartitionSpec as P

HEADS = 6
LANES = 128
FEAT = ("chip", "core")
ALL = ("groups", "chip", "core")
F32 = jnp.float32
BF16 = jnp.bfloat16
NT = (((1,), (1,)), ((), ()))


def unpack(ref_rows, high_rows, side):
    low = ref_rows.astype(F32)
    high = high_rows.astype(F32)
    half = high.shape[-1] // 2
    low = low.reshape(-1, low.shape[-1])
    high = high.reshape(-1, high.shape[-1])
    return jnp.concatenate([low, high[:, side * half : (side + 1) * half]], axis=-1)


def normed_by(values, gain):
    width = values.shape[-1]
    mean = jnp.sum(values, axis=-1, keepdims=True) * (1.0 / width)
    centered = values - mean
    var = jnp.sum(centered * centered, axis=-1, keepdims=True) * (1.0 / width)
    return centered * lax.rsqrt(var + 1e-05) * gain


def pack_kernel(rows, ids_ref, cells_ref, missing_ref, table_ref, nan_ref, out_ref):
    feats, width = cells_ref.shape[1:]
    femb = jnp.concatenate([table_ref[pl.ds(ids_ref[f], 1), :] for f in range(feats)], axis=0)
    nan = nan_ref[...]
    chips = out_ref.shape[0]

    def tokens(r):
        column = missing_ref[:, r : r + 1].astype(F32)
        return cells_ref[r].astype(F32) + column * nan + femb

    for c in range(chips):
        for p in range(rows // 2):
            one, two = tokens(c * rows + 2 * p), tokens(c * rows + 2 * p + 1)
            both = jnp.concatenate([one[:, :LANES], two[:, :LANES]], axis=0)
            out_ref[c, 2 * p * feats : (2 * p + 2) * feats, :] = both.astype(BF16)
            high = jnp.concatenate([one[:, LANES:], two[:, LANES:]], axis=1)
            start = rows * feats + p * feats
            out_ref[c, start : start + feats, :] = high.astype(BF16)


def attention_kernel(rows, feats, own_ref, other_ref, gain_ref, w_ref, out_ref):
    width = gain_ref.shape[-1]
    head_dim = width // HEADS
    chips = own_ref.shape[0]
    cells = chips * feats
    head_of = lax.broadcasted_iota(jnp.int32, (1, width), 1) // head_dim
    scale = head_dim**-0.5 * 1.4426950408889634
    gain = gain_ref[...]

    @pl.loop(0, rows // 2)
    def _(p):
        highs = [r[:, pl.ds(pl.multiple_of((rows + p) * feats, feats), feats), :] for r in (own_ref, other_ref)]
        contexts = []
        for side in range(2):
            at = pl.ds(pl.multiple_of((2 * p + side) * feats, feats), feats)
            values = jnp.concatenate(
                [unpack(r[:, at, :], h, side) for r, h in zip((own_ref, other_ref), highs)], axis=0
            )
            normed = normed_by(values, gain).astype(BF16)
            q = jnp.dot(normed[:cells], w_ref[:, :width], preferred_element_type=F32)
            k = jnp.dot(normed, w_ref[:, width : 2 * width], preferred_element_type=F32).astype(BF16)
            v = jnp.dot(normed, w_ref[:, 2 * width :], preferred_element_type=F32).astype(BF16)
            q = q.astype(BF16)
            context = jnp.zeros((cells, width), F32)
            for h in range(HEADS):
                mine = head_of == h
                scores = lax.dot_general(
                    jnp.where(mine, q, jnp.zeros_like(q)), k, NT, preferred_element_type=F32
                )
                top = jnp.max(scores, axis=-1, keepdims=True)
                expo = jnp.exp2((scores - top) * scale)
                total = jnp.sum(expo, axis=-1, keepdims=True)
                part = jnp.dot(expo.astype(BF16), v, preferred_element_type=F32)
                context = jnp.where(mine, part / total, context)
            out_ref[:, at, :] = context[:, :LANES].reshape(chips, feats, LANES).astype(BF16)
            contexts.append(context[:, LANES:])
        high = jnp.concatenate(contexts, axis=1).reshape(chips, feats, LANES)
        out_ref[:, pl.ds(pl.multiple_of((rows + p) * feats, feats), feats), :] = high.astype(BF16)


def finish_kernel(rows, feats, base_ref, context_ref, w_out_ref, gain_ref, w_up_ref, w_down_ref, out_ref):
    width = gain_ref.shape[-1]
    chips = base_ref.shape[0]

    def whole(ref):
        low = ref[:, : rows * feats, :].astype(F32).reshape(chips, rows // 2, 2, feats, LANES)
        high = ref[:, rows * feats :, :].astype(F32).reshape(chips, rows // 2, feats, LANES)
        half = LANES // 2
        sides = [
            jnp.concatenate([low[:, :, s], high[..., s * half : (s + 1) * half]], axis=-1) for s in range(2)
        ]
        return jnp.stack(sides, axis=2).reshape(-1, width)

    context = whole(context_ref).astype(BF16)
    mid = whole(base_ref) + jnp.dot(context, w_out_ref[...], preferred_element_type=F32)
    normed = normed_by(mid, gain_ref[...]).astype(BF16)
    up = jnp.dot(normed, w_up_ref[...], preferred_element_type=F32)
    act = (0.5 * up * (1.0 + lax.erf(up * 0.5**0.5))).astype(BF16)
    out = mid + lax.dot_general(act, w_down_ref[...], NT, preferred_element_type=F32)
    out_ref[...] = out.reshape(out_ref.shape)


def vmem(count):
    return [pl.BlockSpec(memory_space=pltpu.VMEM)] * count


def body(
    cells, missing, feat_ids, feat_table, nan_embed, gain_one, w_qkv, w_out, gain_two, w_up, w_down
):
    chips = lax.axis_size("chip")
    all_rows, feats, width = cells.shape
    rows = all_rows // chips
    packed = jax.ShapeDtypeStruct((chips, rows * feats * width // LANES, LANES), BF16)
    tokens = pl.pallas_call(
        functools.partial(pack_kernel, rows),
        out_shape=packed,
        in_specs=[pl.BlockSpec(memory_space=pltpu.SMEM), *vmem(4)],
        out_specs=vmem(1)[0],
        name="pack",
    )(feat_ids, cells, missing.T, feat_table, nan_embed[None])
    own = lax.all_to_all(tokens, "chip", 0, 0, tiled=True)
    other = lax.ppermute(own, "core", [(0, 1), (1, 0)])
    context = pl.pallas_call(
        functools.partial(attention_kernel, rows, feats),
        out_shape=packed,
        in_specs=vmem(4),
        out_specs=vmem(1)[0],
        name="attend",
    )(own, other, gain_one[None], w_qkv)
    context = lax.all_to_all(context, "chip", 0, 0, tiled=True)
    steps = 4 if chips % 4 == 0 else 1
    block = (chips // steps, *packed.shape[1:])
    whole = lambda shape: pl.BlockSpec(shape, lambda i: (0, 0))
    return pl.pallas_call(
        functools.partial(finish_kernel, rows, feats),
        out_shape=jax.ShapeDtypeStruct(cells.shape, F32),
        grid=(steps,),
        in_specs=[
            pl.BlockSpec(block, lambda i: (i, 0, 0)),
            pl.BlockSpec(block, lambda i: (i, 0, 0)),
            whole(w_out.shape),
            whole((1, width)),
            whole(w_up.shape),
            whole(w_down.shape[::-1]),
        ],
        out_specs=pl.BlockSpec((all_rows // steps, feats, width), lambda i: (i, 0, 0)),
        name="finish",
    )(tokens, context, w_out, gain_two[None], w_up, w_down.T)


def solution(mesh):
    chips = mesh.shape["feat"] // 2
    split = Mesh(mesh.devices.reshape(mesh.shape["groups"], chips, 2), ALL)
    in_specs = (P("groups", FEAT, None), P("groups", FEAT), P(ALL)) + (P(),) * 8
    return jax.shard_map(
        body, mesh=split, in_specs=in_specs, out_specs=P("groups", FEAT, None), check_vma=False
    )
```

time: 266 us -> 204 us (0.77)
  waiting for transfers between devices: 85.7 us -> 1.63 us
  blocking collectives: 119 us -> 178 us
  matrix products: 39.7 us -> 0 us
  Pallas kernels: 0 us -> 21.3 us
  starting transfers between devices: 13.4 us -> 1.38 us
  other arithmetic: 4.23 us -> 0 us
    all_to_all x1 -> x0, waiting for transfers between devices: 85.7 us -> none  [moved_by_axis(): filled = lax.all_to_all(filled, axes[k], k, k, tiled=True)]
    all_to_all x3 -> x2, blocking collectives: 119 us -> 178 us  [the longest x1 103 us: body(): own = lax.all_to_all(tokens, 'chip', 0, 0, tiled=True)]
    dot_general x13 -> x0, matrix products: 25.4 us -> none  [the longest x3 12.2 us: finish(): return mid + jnp.dot(act, w_down, preferred_element_type=jnp.float32)]
    pallas_call x0 -> x3, Pallas kernels: none -> 21.3 us  [the longest x1 12.3 us: body(): pl.pallas_call(functools.partial(attention_kernel, rows, feats), out_shap...]
    sub x3 -> x0, matrix products: 14.3 us -> none  [attend(): expo = jnp.exp(scores - top)]
    all_to_all x1 -> x0, starting transfers between devices: 13.4 us -> none  [moved_by_axis(): filled = lax.all_to_all(filled, axes[k], k, k, tiled=True)]
    convert_element_type x3 -> x0, other arithmetic: 3.53 us -> none  [the longest x1 1.49 us: body(): tokens = (cells.astype(jnp.float32) + missing[..., None].astype(jnp.float...]
where the time goes in v1:
time: 204 us; the launch traced here: 203 us
  blocking collectives  178 us (87%)
  Pallas kernels  21.3 us (10%)
    all_to_all x1, blocking collectives, body(): own = lax.all_to_all(tokens, 'chip', 0, 0, tiled=True)  103 us
    all_to_all x1, blocking collectives, body(): context = lax.all_to_all(context, 'chip', 0, 0, tiled=True)  75.4 us
    pallas_call x1, Pallas kernels, body(): pl.pallas_call(functools.partial(attention_kernel, rows, feats), out_shap...  12.3 us
    pallas_call x1, Pallas kernels, body(): pl.pallas_call(functools.partial(finish_kernel, rows, feats), out_shape=j...  6.29 us
  transfers between devices with their start and end apart: 1, of which 1 were waited for; matrix products, arithmetic and copies ran while one was open for 0% of the time, Pallas kernels for 0%

profile of v1, /device:TPU:37, one launch (start us, length us, event | category | flops | bytes accessed | tf_op | source)
XLA Modules:
  0.0 203.3 jit_solution(16958994204575189135)
XLA Ops:
  0.0 2.7 %pack.1.base_ref = bf16[32,72,128]{2,1,0:T(8,128)(2,1)} custom-call(s32[8]{0:T(128)} %ids_ref.1, bf16[192,8,192]{2,1,0:T(8,128)(2,1)} %cells_ref.1, s32[8,192]{1,0:T(8,128)} %bitcast.6, f32[64,192]{1,0:T(8,128)} %table_ref.1, f32[1,192]{1,0:T(1,128)} %bitcast.9), custom_call_target="tpu_custom_call" | custom-call | tf_op jit(solution)/shard_map/pack/pallas_call | solution.py:130
  2.7 102.7 %all_to_all.10.own_ref = bf16[32,72,128]{2,1,0:T(8,128)(2,1)S(1)} all-to-all(bf16[32,72,128]{2,1,0:T(8,128)(2,1)} %pack.1.base_ref), channel_id=1, replica_groups=mesh['groups'=4,'chip'=32,'core'=2] {'chip'}, dimensions={0} | all-to-all | bytes 1179648 | tf_op jit(solution)/shard_map/all_to_all | solution.py:137
  105.4 0.0 copy-start
  105.4 1.4 collective-permute-start
  106.7 1.6 collective-permute-done.other_ref
  108.4 0.0 copy-start.1
  108.4 0.0 copy-done
  108.4 0.9 copy-done.1
  109.2 12.3 %attend.1 = bf16[32,72,128]{2,1,0:T(8,128)(2,1)} custom-call(bf16[32,72,128]{2,1,0:T(8,128)(2,1)} %copy-done, bf16[32,72,128]{2,1,0:T(8,128)(2,1)} %copy-done.1, f32[1,192]{1,0:T(1,128)} %bitcast.7, bf16[192,576]{1,0:T(8,128)(2,1)} %w_ref.1), custom_call_target="tpu_custom_call" | custom-call | tf_op jit(solution)/shard_map/attend/pallas_call | solution.py:139
  121.6 75.4 %all_to_all.11.context_ref = bf16[32,72,128]{2,1,0:T(8,128)(2,1)} all-to-all(bf16[32,72,128]{2,1,0:T(8,128)(2,1)} %attend.1), channel_id=1, replica_groups=mesh['groups'=4,'chip'=32,'core'=2] {'chip'}, dimensions={0} | all-to-all | bytes 1179648 | tf_op jit(solution)/shard_map/all_to_all | solution.py:146
  197.0 6.3 %finish.1 = f32[192,8,192]{2,1,0:T(8,128)} custom-call(bf16[32,72,128]{2,1,0:T(8,128)(2,1)} %pack.1.base_ref, bf16[32,72,128]{2,1,0:T(8,128)(2,1)} %all_to_all.11.context_ref, bf16[192,192]{1,0:T(8,128)(2,1)} %w_out_ref.1, f32[1,192]{1,0:T(1,128)} %bitcast.8, bf16[192,768]{1,0:T(8,128)(2,1)} %w_up_ref.1, bf16[192,768]{1,0:T(8,128)(2,1)} %bitcast.5), custom_call_target="tpu_custom_call" | custom-call | tf_op jit(solution)/shard_map/finish/pallas_call | solution.py:150
Async XLA Ops:
  105.4 3.0 %copy-start = (bf16[32,72,128]{2,1,0:T(8,128)(2,1)}, bf16[32,72,128]{2,1,0:T(8,128)(2,1)S(1)}, u32[]{:S(2)}) copy-start(bf16[32,72,128]{2,1,0:T(8,128)(2,1)S(1)} %all_to_all.10.own_ref) | copy-start | bytes 1769476
  105.4 3.0 %collective-permute-start = (bf16[32,72,128]{2,1,0:T(8,128)(2,1)S(1)}, bf16[32,72,128]{2,1,0:T(8,128)(2,1)S(1)}, u32[]{:S(2)}, u32[]{:S(2)}) collective-permute-start(bf16[32,72,128]{2,1,0:T(8,128)(2,1)S(1)} %all_to_all.10.own_ref), channel_id=1, source_target_pairs={{0,1},{1,0},{2,3},{3,2},{4,5},{5,4},{6,7},{7,6},{8,9},{9,8},{10,11... | collective-permute-start | bytes 1769480 | tf_op jit(solution)/shard_map/ppermute | solution.py:138
  108.4 0.9 copy-start.1

commit v2 on v1

v2 whole, which is shorter than its diff:
```python
import functools

import jax
import jax.numpy as jnp
from jax import lax
from jax.experimental import pallas as pl
from jax.experimental.pallas import tpu as pltpu
from jax.sharding import Mesh
from jax.sharding import PartitionSpec as P

HEADS = 6
LANES = 128
ONES = 16
LEAD, LAG = 2, 1
HOLD_NS = 27000
FEAT = ("chip", "core")
ALL = ("groups", "chip", "core")
F32 = jnp.float32
BF16 = jnp.bfloat16
NT = (((1,), (1,)), ((), ()))


def normed_by(values, gain):
    width = values.shape[-1]
    mean = jnp.sum(values, axis=-1, keepdims=True) * (1.0 / width)
    centered = values - mean
    var = jnp.sum(centered * centered, axis=-1, keepdims=True) * (1.0 / width)
    return centered * lax.rsqrt(var + 1e-05) * gain


def tokens_kernel(chips, cells_ref, missing_ref, table_ref, nan_ref, ids_ref, own_ref, other_ref):
    feats = cells_ref.shape[1]
    rows = cells_ref.shape[0] // chips
    half = rows // 2
    core = lax.axis_index("core")
    femb = jnp.concatenate([table_ref[pl.ds(ids_ref[f], 1), :] for f in range(feats)], axis=0)
    nan = nan_ref[...]
    low = missing_ref[...].astype(F32)
    high = jnp.concatenate([low[:, half:], low[:, :half]], axis=1)
    for j, out_ref in enumerate((own_ref, other_ref)):
        of_core = core if j == 0 else 1 - core
        column = jnp.where(of_core == 0, low, high)
        for c in range(chips):
            for i in range(half):
                lane = c * rows + i
                cell = cells_ref[lane + of_core * half].astype(F32)
                out_ref[c * half + i] = (cell + column[:, lane : lane + 1] * nan + femb).astype(BF16)


def merge_kernel(own_ref, other_ref, out_ref):
    chips = out_ref.shape[0]
    half = own_ref.shape[0] // chips
    feats = own_ref.shape[1]

    @pl.when(lax.axis_index("core") == 1)
    def _():
        pl.delay(HOLD_NS)

    for c in range(chips):
        for i in range(half):
            own = own_ref[c * half + i].astype(F32)
            other = other_ref[c * half + i].astype(F32)
            low = jnp.concatenate([own[:, :LANES], other[:, :LANES]], axis=0).astype(BF16)
            high = jnp.concatenate([own[:, LANES:], other[:, LANES:]], axis=1).astype(BF16)
            out_ref[c, 3 * i * feats : (3 * i + 2) * feats, :] = low
            out_ref[c, (3 * i + 2) * feats : (3 * i + 3) * feats, :] = high


def attention_kernel(feats, in_ref, gain_ref, w_ref, w_v_ref, out_ref):
    width = gain_ref.shape[-1]
    head_dim = width // HEADS
    chips = in_ref.shape[0]
    cells = chips * feats
    split = LANES // 2
    head_of = lax.broadcasted_iota(jnp.int32, (1, width), 1) // head_dim
    scale = head_dim**-0.5 * 1.4426950408889634
    gain = gain_ref[...]

    def tile(i, t):
        return pl.ds(pl.multiple_of((3 * i + t) * feats, feats), feats)

    def flat(i, t):
        return in_ref[:, tile(i, t), :].astype(F32).reshape(cells, LANES)

    def scores_of(q, k, h):
        mine = jnp.where(head_of == h, q, jnp.zeros_like(q))
        return lax.dot_general(k, mine, NT, preferred_element_type=F32)

    def softmax(s):
        top = jnp.max(s, axis=0, keepdims=True)
        return jnp.exp2((s - top) * scale).astype(BF16)

    def context_of(v, expo, h):
        mine = v[h * head_dim : (h + 1) * head_dim]
        mine = jnp.concatenate([mine, jnp.ones((ONES, 2 * cells), BF16)], axis=0)
        part = jnp.dot(mine, expo, preferred_element_type=F32)
        return part[:head_dim] * (1.0 / part[head_dim : head_dim + 1])

    @pl.loop(0, in_ref.shape[1] // (3 * feats))
    def _(i):
        high = flat(i, 2)
        values = jnp.concatenate(
            [
                jnp.concatenate([flat(i, side), high[:, side * split : (side + 1) * split]], axis=1)
                for side in range(2)
            ],
            axis=0,
        )
        normed = normed_by(values, gain).astype(BF16)
        q = jnp.dot(normed, w_ref[:, :width], preferred_element_type=F32).astype(BF16)
        k = jnp.dot(normed, w_ref[:, width:], preferred_element_type=F32).astype(BF16)
        v = lax.dot_general(w_v_ref[...], normed, NT, preferred_element_type=F32).astype(BF16)
        sides = [q[:cells], q[cells:]]
        pairs = [(h, side) for h in range(HEADS) for side in range(2)]
        ahead = [scores_of(sides[side], k, h) for h, side in pairs[:LEAD]]
        done = [[], []]
        expos = []
        for n, (h, side) in enumerate(pairs):
            if n + LEAD < len(pairs):
                h2, side2 = pairs[n + LEAD]
                ahead.append(scores_of(sides[side2], k, h2))
            expos.append(softmax(ahead.pop(0)))
            if n >= LAG:
                h0, side0 = pairs[n - LAG]
                done[side0].append(context_of(v, expos.pop(0), h0))
        for h0, side0 in pairs[len(pairs) - LAG :]:
            done[side0].append(context_of(v, expos.pop(0), h0))
        highs = []
        for side in range(2):
            done[side].append(jnp.zeros((2 * LANES - width, cells), F32))
            context = jnp.concatenate(done[side], axis=0).T
            out_ref[:, tile(i, side), :] = context[:, :LANES].reshape(chips, feats, LANES).astype(BF16)
            highs.append(context[:, LANES:width])
        high = jnp.concatenate(highs, axis=1).reshape(chips, feats, LANES)
        out_ref[:, tile(i, 2), :] = high.astype(BF16)


def finish_kernel(
    feats, own_base_ref, other_base_ref, own_ref, other_ref, w_out_ref, gain_ref, w_up_ref, w_down_ref, out_ref
):
    width = gain_ref.shape[-1]
    chips = own_ref.shape[0]
    half = own_ref.shape[1] // (3 * feats)
    split = LANES // 2
    core = lax.axis_index("core")
    for j, (base_ref, context_ref) in enumerate(((own_base_ref, own_ref), (other_base_ref, other_ref))):
        tiles = context_ref[...].astype(F32).reshape(chips, half, 3, feats, LANES)
        context = jnp.concatenate([tiles[:, :, j], tiles[:, :, 2, :, j * split : (j + 1) * split]], axis=-1)
        context = context.reshape(-1, width).astype(BF16)
        base = base_ref[...].astype(F32).reshape(-1, width)
        mid = base + jnp.dot(context, w_out_ref[...], preferred_element_type=F32)
        normed = normed_by(mid, gain_ref[...]).astype(BF16)
        up = jnp.dot(normed, w_up_ref[...], preferred_element_type=F32)
        act = (0.5 * up * (1.0 + lax.erf(up * 0.5**0.5))).astype(BF16)
        out = mid + lax.dot_general(act, w_down_ref[...], NT, preferred_element_type=F32)
        out = out.reshape(chips, half, feats, width)
        of_core = core if j == 0 else 1 - core
        for c in range(chips):
            out_ref[pl.ds(c * 2 * half + of_core * half, half)] = out[c]


def vmem(count):
    return [pl.BlockSpec(memory_space=pltpu.VMEM)] * count


def limit(mib):
    return pltpu.CompilerParams(vmem_limit_bytes=mib << 20)


def body(
    cells, missing, feat_ids, feat_table, nan_embed, gain_one, w_qkv, w_out, gain_two, w_up, w_down
):
    chips = lax.axis_size("chip")
    all_rows, feats, width = cells.shape
    swap = [(0, 1), (1, 0)]
    halves = jax.ShapeDtypeStruct((all_rows // 2, feats, width), BF16)
    packed = jax.ShapeDtypeStruct((chips, all_rows * feats * width // (chips * LANES), LANES), BF16)
    own, other = pl.pallas_call(
        functools.partial(tokens_kernel, chips),
        out_shape=[halves] * 2,
        in_specs=[*vmem(4), pl.BlockSpec(memory_space=pltpu.SMEM)],
        out_specs=vmem(2),
        name="tokens",
    )(cells, missing.T, feat_table, nan_embed[None], feat_ids)
    tokens = pl.pallas_call(
        merge_kernel,
        out_shape=packed,
        in_specs=vmem(2),
        out_specs=vmem(1)[0],
        compiler_params=limit(12),
        name="merge",
    )(own, lax.ppermute(other, "core", swap))
    tokens = lax.all_to_all(tokens, "chip", 0, 0, tiled=True)
    context = pl.pallas_call(
        functools.partial(attention_kernel, feats),
        out_shape=packed,
        in_specs=vmem(4),
        out_specs=vmem(1)[0],
        compiler_params=limit(24),
        name="attend",
    )(tokens, gain_one[None], w_qkv[:, : 2 * width], w_qkv[:, 2 * width :].T)
    context = lax.all_to_all(context, "chip", 0, 0, tiled=True)
    steps = 4 if chips % 4 == 0 else 1
    some = pl.BlockSpec((chips // steps, *packed.shape[1:]), lambda n: (n, 0, 0))
    base = pl.BlockSpec((all_rows // 2 // steps, feats, width), lambda n: (n, 0, 0))
    whole = lambda shape: pl.BlockSpec(shape, lambda n: (0, 0))
    return pl.pallas_call(
        functools.partial(finish_kernel, feats),
        out_shape=jax.ShapeDtypeStruct(cells.shape, F32),
        grid=(steps,),
        in_specs=[
            *[base] * 2,
            *[some] * 2,
            whole(w_out.shape),
            whole((1, width)),
            whole(w_up.shape),
            whole(w_down.shape[::-1]),
        ],
        out_specs=pl.BlockSpec((all_rows // steps, feats, width), lambda n: (n, 0, 0)),
        compiler_params=limit(16),
        name="finish",
    )(own, other, context, lax.ppermute(context, "core", swap), w_out, gain_two[None], w_up, w_down.T)


def solution(mesh):
    chips = mesh.shape["feat"] // 2
    split = Mesh(mesh.devices.reshape(mesh.shape["groups"], chips, 2), ALL)
    in_specs = (P("groups", FEAT, None), P("groups", FEAT), P(ALL)) + (P(),) * 8
    return jax.shard_map(
        body, mesh=split, in_specs=in_specs, out_specs=P("groups", FEAT, None), check_vma=False
    )
```

time: 204 us -> 178 us (0.87)
  blocking collectives: 178 us -> 50.4 us
  waiting for transfers between devices: 1.63 us -> 47.3 us
  starting transfers between devices: 1.38 us -> 33.8 us
  Pallas kernels: 21.3 us -> 44.6 us
    all_to_all x1 -> x0, blocking collectives: 103 us -> none  [body(): own = lax.all_to_all(tokens, 'chip', 0, 0, tiled=True)]
    all_to_all x0 -> x1, waiting for transfers between devices: none -> 43.7 us  [body(): tokens = lax.all_to_all(tokens, 'chip', 0, 0, tiled=True)]
    all_to_all x1, blocking collectives: 75.4 us -> 50.4 us  [body(): context = lax.all_to_all(context, 'chip', 0, 0, tiled=True)]
    pallas_call x3 -> x4, Pallas kernels: 21.3 us -> 44.6 us  [the longest x1 27.9 us: body(): pl.pallas_call(merge_kernel, out_shape=packed, in_specs=vmem(2), out_spec...]
    ppermute x1 -> x2, starting transfers between devices: 1.38 us -> 20.4 us  [the longest x1 20.4 us: body(): lax.ppermute(other, 'core', swap)]
    all_to_all x0 -> x1, starting transfers between devices: none -> 13.4 us  [body(): tokens = lax.all_to_all(tokens, 'chip', 0, 0, tiled=True)]
  transfers between devices with their start and end apart: 1 -> 3, of which waited for: 1 -> 3; matrix products, arithmetic and copies ran while one was open for 0% -> 0% of each run, Pallas kernels for 0% -> 0%
where the time goes in v2:
time: 178 us; the launch traced here: 177 us
  blocking collectives  50.4 us (28%)
  waiting for transfers between devices  47.3 us (27%)
  Pallas kernels  44.6 us (25%)
  starting transfers between devices  33.8 us (19%)
    all_to_all x1, blocking collectives, body(): context = lax.all_to_all(context, 'chip', 0, 0, tiled=True)  50.4 us
    all_to_all x1, waiting for transfers between devices, body(): tokens = lax.all_to_all(tokens, 'chip', 0, 0, tiled=True)  43.7 us
    pallas_call x1, Pallas kernels, body(): pl.pallas_call(merge_kernel, out_shape=packed, in_specs=vmem(2), out_spec...  27.9 us
    ppermute x1, starting transfers between devices, body(): lax.ppermute(other, 'core', swap)  20.4 us
    all_to_all x1, starting transfers between devices, body(): tokens = lax.all_to_all(tokens, 'chip', 0, 0, tiled=True)  13.4 us
    pallas_call x1, Pallas kernels, body(): pl.pallas_call(functools.partial(attention_kernel, feats), out_shape=pack...  8.8 us
    pallas_call x1, Pallas kernels, body(): pl.pallas_call(functools.partial(finish_kernel, feats), out_shape=jax.Sha...  5.41 us
  transfers between devices with their start and end apart: 3, of which 3 were waited for; matrix products, arithmetic and copies ran while one was open for 0% of the time, Pallas kernels for 0%

profile of v2, /device:TPU:37, one launch (start us, length us, event | category | flops | bytes accessed | tf_op | source)
XLA Modules:
  0.0 177.4 jit_solution(2013630183997292211)
XLA Ops:
  0.0 0.0 copy-start.8
  0.0 0.0 slice-start
  0.0 2.4 %tokens.1 = (bf16[96,8,192]{2,1,0:T(8,128)(2,1)}, bf16[96,8,192]{2,1,0:T(8,128)(2,1)}) custom-call(bf16[192,8,192]{2,1,0:T(8,128)(2,1)} %cells_ref.1, s32[8,192]{1,0:T(8,128)} %bitcast.10, f32[64,192]{1,0:T(8,128)} %table_ref.1, f32[1,192]{1,0:T(1,128)} %bitcast.11, s32[8]{0:T(128)} %ids_ref.1), custom_call_target="tpu_custom_call" | custom-call | tf_op jit(solution)/shard_map/tokens/pallas_call | solution.py:178
  2.5 20.4 %collective-permute-start = (bf16[96,8,192]{2,1,0:T(8,128)(2,1)}, bf16[96,8,192]{2,1,0:T(8,128)(2,1)S(1)}, u32[]{:S(2)}, u32[]{:S(2)}) collective-permute-start(bf16[96,8,192]{2,1,0:T(8,128)(2,1)} %get-tuple-element.8.other_base_ref), channel_id=1, source_target_pairs={{0,1},{1,0},{2,3},{3,2},{4,5},{5,4},{6,7},{7,6},{8,9},{9,8},{10,11... | collective-permute-start | bytes 884744 | tf_op jit(solution)/shard_map/ppermute | solution.py:192
  22.9 1.6 collective-permute-done.other_ref
  24.4 0.0 copy-start
  24.4 1.0 copy-done
  25.4 0.0 copy-start.6
  25.4 27.9 %merge.1 = bf16[32,72,128]{2,1,0:T(8,128)(2,1)} custom-call(bf16[96,8,192]{2,1,0:T(8,128)(2,1)S(1)} %copy-done, bf16[96,8,192]{2,1,0:T(8,128)(2,1)S(1)} %collective-permute-done.other_ref), custom_call_target="tpu_custom_call" | custom-call | tf_op jit(solution)/shard_map/merge/pallas_call | solution.py:185
  53.4 13.4 %all-to-all-start = ((bf16[32,72,128]{2,1,0:T(8,128)(2,1)}), bf16[32,72,128]{2,1,0:T(8,128)(2,1)S(1)}, u32[]{:S(2)}, u32[]{:S(2)}) async-start(bf16[32,72,128]{2,1,0:T(8,128)(2,1)} %merge.1), calls=%async_computation | async-start | bytes 1179648 | tf_op jit(solution)/shard_map/all_to_all | solution.py:193
  66.8 0.0 copy-done.8
  66.8 0.0 copy-start.1
  66.8 0.0 copy-start.2
  66.8 0.0 copy-start.3
  66.8 0.0 copy-start.4
  66.8 0.0 copy-start.5
  66.8 0.0 copy-start.7
  66.9 0.0 slice-done
  66.9 0.1 copy.13
  67.0 43.7 %all-to-all-done.in_ref = bf16[32,72,128]{2,1,0:T(8,128)(2,1)S(1)} async-done(((bf16[32,72,128]{2,1,0:T(8,128)(2,1)}), bf16[32,72,128]{2,1,0:T(8,128)(2,1)S(1)}, u32[]{:S(2)}, u32[]{:S(2)}) %all-to-all-start) | async-done | bytes 589856 | tf_op jit(solution)/shard_map/all_to_all | solution.py:193
  110.7 0.0 copy-done.6
  110.7 8.8 %attend.1 = bf16[32,72,128]{2,1,0:T(8,128)(2,1)S(1)} custom-call(bf16[32,72,128]{2,1,0:T(8,128)(2,1)S(1)} %all-to-all-done.in_ref, f32[1,192]{1,0:T(1,128)S(1)} %bitcast.8, bf16[192,384]{1,0:T(8,128)(2,1)S(1)} %slice.6.w_ref, bf16[192,192]{1,0:T(8,128)(2,1)S(1)} %bitcast.6), custom_call_target="tpu_custom_call" | custom-call | tf_op jit(solution)/shard_map/attend/pallas_call | solution.py:194
  119.5 50.4 %all_to_all.10.own_ref = bf16[32,72,128]{2,1,0:T(8,128)(2,1)S(1)} all-to-all(bf16[32,72,128]{2,1,0:T(8,128)(2,1)S(1)} %attend.1), channel_id=1, replica_groups=mesh['groups'=4,'chip'=32,'core'=2] {'chip'}, dimensions={0} | all-to-all | bytes 1179648 | tf_op jit(solution)/shard_map/all_to_all | solution.py:202
  169.9 0.0 collective-permute-start.1
  170.0 2.0 %collective-permute-done.1.other_ref = bf16[32,72,128]{2,1,0:T(8,128)(2,1)S(1)} collective-permute-done((bf16[32,72,128]{2,1,0:T(8,128)(2,1)S(1)}, bf16[32,72,128]{2,1,0:T(8,128)(2,1)S(1)}, u32[]{:S(2)}, u32[]{:S(2)}) %collective-permute-start.1) | collective-permute-done | bytes 589856 | tf_op jit(solution)/shard_map/ppermute | solution.py:222
  172.0 0.0 copy-done.1
  172.0 0.0 copy-done.2
  172.0 0.0 copy-done.3
  172.0 0.0 copy-done.4
  172.0 0.0 copy-done.5
  172.0 0.0 copy-done.7
  172.0 5.4 %finish.1 = f32[192,8,192]{2,1,0:T(8,128)} custom-call(bf16[96,8,192]{2,1,0:T(8,128)(2,1)S(1)} %copy-done.1, bf16[96,8,192]{2,1,0:T(8,128)(2,1)S(1)} %copy-done.2, bf16[32,72,128]{2,1,0:T(8,128)(2,1)S(1)} %all_to_all.10.own_ref, bf16[32,72,128]{2,1,0:T(8,128)(2,1)S(1)} %collective-permute-done.1.other_ref, bf16[192,192]{1,0:T(8,128)(2,1)S(1)} %copy-done.5, ...), custom_call_target="tpu_custom_call" | custom-call | tf_op jit(solution)/shard_map/finish/pallas_call | solution.py:207
  (1 shorter events, 0.0 us)
Async XLA Ops:
  0.0 66.8 %copy-start.8 = (bf16[192,576]{1,0:T(8,128)(2,1)S(1)}, bf16[192,576]{1,0:T(8,128)(2,1)}, u32[]{:S(2)}) copy-start(bf16[192,576]{1,0:T(8,128)(2,1)} %param.17) | copy-start | bytes 663556
  0.0 66.9 %slice-start = ((bf16[192,576]{1,0:T(8,128)(2,1)}), bf16[192,192]{1,0:T(8,128)(2,1)S(1)}, s32[]{:S(2)}) async-start(bf16[192,576]{1,0:T(8,128)(2,1)} %param.17), calls=%async_computation.2 | async-start | bytes 196608 | tf_op jit(solution)/shard_map/slice | solution.py:201
  2.5 22.0 %collective-permute-start = (bf16[96,8,192]{2,1,0:T(8,128)(2,1)}, bf16[96,8,192]{2,1,0:T(8,128)(2,1)S(1)}, u32[]{:S(2)}, u32[]{:S(2)}) collective-permute-start(bf16[96,8,192]{2,1,0:T(8,128)(2,1)} %get-tuple-element.8.other_base_ref), channel_id=1, source_target_pairs={{0,1},{1,0},{2,3},{3,2},{4,5},{5,4},{6,7},{7,6},{8,9},{9,8},{10,11... | collective-permute-start | bytes 884744 | tf_op jit(solution)/shard_map/ppermute | solution.py:192
  24.4 1.0 copy-start
  25.4 85.3 %copy-start.6 = (f32[192]{0:T(256)S(1)}, f32[192]{0:T(256)}, u32[]{:S(2)}) copy-start(f32[192]{0:T(256)} %param.16) | copy-start | bytes 2308
  53.4 57.4 %all-to-all-start = ((bf16[32,72,128]{2,1,0:T(8,128)(2,1)}), bf16[32,72,128]{2,1,0:T(8,128)(2,1)S(1)}, u32[]{:S(2)}, u32[]{:S(2)}) async-start(bf16[32,72,128]{2,1,0:T(8,128)(2,1)} %merge.1), calls=%async_computation | async-start | bytes 1179648 | tf_op jit(solution)/shard_map/all_to_all | solution.py:193
  66.8 105.2 %copy-start.1 = (bf16[96,8,192]{2,1,0:T(8,128)(2,1)S(1)}, bf16[96,8,192]{2,1,0:T(8,128)(2,1)}, u32[]{:S(2)}) copy-start(bf16[96,8,192]{2,1,0:T(8,128)(2,1)} %get-tuple-element.7.own_ref.own_base_ref) | copy-start | bytes 884740
  66.8 105.2 %copy-start.2 = (bf16[96,8,192]{2,1,0:T(8,128)(2,1)S(1)}, bf16[96,8,192]{2,1,0:T(8,128)(2,1)}, u32[]{:S(2)}) copy-start(bf16[96,8,192]{2,1,0:T(8,128)(2,1)} %get-tuple-element.8.other_base_ref) | copy-start | bytes 884740
  66.8 105.2 %copy-start.3 = (bf16[192,768]{1,0:T(8,128)(2,1)S(1)}, bf16[192,768]{1,0:T(8,128)(2,1)}, u32[]{:S(2)}) copy-start(bf16[192,768]{1,0:T(8,128)(2,1)} %w_up_ref.1) | copy-start | bytes 884740
  66.8 105.2 %copy-start.4 = (bf16[768,192]{0,1:T(8,128)(2,1)S(1)}, bf16[768,192]{0,1:T(8,128)(2,1)}, u32[]{:S(2)}) copy-start(bf16[768,192]{0,1:T(8,128)(2,1)} %param.21) | copy-start | bytes 884740
  66.8 105.2 %copy-start.5 = (bf16[192,192]{1,0:T(8,128)(2,1)S(1)}, bf16[192,192]{1,0:T(8,128)(2,1)}, u32[]{:S(2)}) copy-start(bf16[192,192]{1,0:T(8,128)(2,1)} %w_out_ref.1) | copy-start | bytes 221188
  66.8 105.2 %copy-start.7 = (f32[192]{0:T(256)S(1)}, f32[192]{0:T(256)}, u32[]{:S(2)}) copy-start(f32[192]{0:T(256)} %param.19) | copy-start | bytes 2308
  169.9 2.0 %collective-permute-start.1 = (bf16[32,72,128]{2,1,0:T(8,128)(2,1)S(1)}, bf16[32,72,128]{2,1,0:T(8,128)(2,1)S(1)}, u32[]{:S(2)}, u32[]{:S(2)}) collective-permute-start(bf16[32,72,128]{2,1,0:T(8,128)(2,1)S(1)} %all_to_all.10.own_ref), channel_id=1, source_target_pairs={{0,1},{1,0},{2,3},{3,2},{4,5},{5,4},{6,7},{7,6},{8,9},{9,8},{10,11... | collective-permute-start | bytes 1769480 | tf_op jit(solution)/shard_map/ppermute | solution.py:222

commit v3 on v2

--- a/solution.py
+++ b/solution.py
@@ -12,12 +12,14 @@
 LANES = 128
 ONES = 16
 LEAD, LAG = 2, 1
-HOLD_NS = 27000
+HOLD_NS = 28000
+PIECES = 4
 FEAT = ("chip", "core")
 ALL = ("groups", "chip", "core")
 F32 = jnp.float32
 BF16 = jnp.bfloat16
 NT = (((1,), (1,)), ((), ()))
+TT = (((0,), (1,)), ((), ()))
 
 
 def normed_by(values, gain):
@@ -28,19 +30,40 @@
     return centered * lax.rsqrt(var + 1e-05) * gain
 
 
-def tokens_kernel(chips, cells_ref, missing_ref, table_ref, nan_ref, ids_ref, own_ref, other_ref):
+def tokens_kernel(
+    chips, cells_hbm, missing_hbm, table_hbm, nan_hbm, ids_hbm, own_ref, other_ref,
+    cells_ref, missing_ref, table_ref, nan_ref, ids_ref, sems
+):
     feats = cells_ref.shape[1]
     rows = cells_ref.shape[0] // chips
     half = rows // 2
+    part = cells_ref.shape[0] // PIECES
     core = lax.axis_index("core")
+    small = [
+        pltpu.make_async_copy(*pair, sems.at[n])
+        for n, pair in enumerate(
+            [(ids_hbm, ids_ref), (table_hbm, table_ref), (missing_hbm, missing_ref), (nan_hbm, nan_ref)]
+        )
+    ]
+    large = [
+        pltpu.make_async_copy(
+            cells_hbm.at[pl.ds(n * part, part)], cells_ref.at[pl.ds(n * part, part)], sems.at[len(small) + n]
+        )
+        for n in range(PIECES)
+    ]
+    for copy in small + large:
+        copy.start()
+    for copy in small:
+        copy.wait()
     femb = jnp.concatenate([table_ref[pl.ds(ids_ref[f], 1), :] for f in range(feats)], axis=0)
     nan = nan_ref[...]
     low = missing_ref[...].astype(F32)
     high = jnp.concatenate([low[:, half:], low[:, :half]], axis=1)
-    for j, out_ref in enumerate((own_ref, other_ref)):
-        of_core = core if j == 0 else 1 - core
-        column = jnp.where(of_core == 0, low, high)
-        for c in range(chips):
+    columns = [jnp.where(c == 0, low, high) for c in (core, 1 - core)]
+    for c in range(chips):
+        if c % (chips // PIECES) == 0:
+            large[c // (chips // PIECES)].wait()
+        for of_core, column, out_ref in ((core, columns[0], own_ref), (1 - core, columns[1], other_ref)):
             for i in range(half):
                 lane = c * rows + i
                 cell = cells_ref[lane + of_core * half].astype(F32)
@@ -66,7 +89,7 @@
             out_ref[c, (3 * i + 2) * feats : (3 * i + 3) * feats, :] = high
 
 
-def attention_kernel(feats, in_ref, gain_ref, w_ref, w_v_ref, out_ref):
+def attention_kernel(feats, in_ref, gain_ref, w_ref, out_ref):
     width = gain_ref.shape[-1]
     head_dim = width // HEADS
     chips = in_ref.shape[0]
@@ -108,8 +131,8 @@
         )
         normed = normed_by(values, gain).astype(BF16)
         q = jnp.dot(normed, w_ref[:, :width], preferred_element_type=F32).astype(BF16)
-        k = jnp.dot(normed, w_ref[:, width:], preferred_element_type=F32).astype(BF16)
-        v = lax.dot_general(w_v_ref[...], normed, NT, preferred_element_type=F32).astype(BF16)
+        k = jnp.dot(normed, w_ref[:, width : 2 * width], preferred_element_type=F32).astype(BF16)
+        v = lax.dot_general(w_ref[:, 2 * width :], normed, TT, preferred_element_type=F32).astype(BF16)
         sides = [q[:cells], q[cells:]]
         pairs = [(h, side) for h in range(HEADS) for side in range(2)]
         ahead = [scores_of(sides[side], k, h) for h, side in pairs[:LEAD]]
@@ -136,27 +159,33 @@
 
 
 def finish_kernel(
-    feats, own_base_ref, other_base_ref, own_ref, other_ref, w_out_ref, gain_ref, w_up_ref, w_down_ref, out_ref
+    feats, of_other, base_ref, context_ref, w_out_ref, gain_ref, w_up_ref, w_down_ref, *rest
 ):
+    out_hbm, held_ref, sems = rest[-3:]
     width = gain_ref.shape[-1]
-    chips = own_ref.shape[0]
-    half = own_ref.shape[1] // (3 * feats)
+    chips = context_ref.shape[0]
+    half = context_ref.shape[1] // (3 * feats)
     split = LANES // 2
     core = lax.axis_index("core")
-    for j, (base_ref, context_ref) in enumerate(((own_base_ref, own_ref), (other_base_ref, other_ref))):
-        tiles = context_ref[...].astype(F32).reshape(chips, half, 3, feats, LANES)
-        context = jnp.concatenate([tiles[:, :, j], tiles[:, :, 2, :, j * split : (j + 1) * split]], axis=-1)
-        context = context.reshape(-1, width).astype(BF16)
-        base = base_ref[...].astype(F32).reshape(-1, width)
-        mid = base + jnp.dot(context, w_out_ref[...], preferred_element_type=F32)
+    of_core = 1 - core if of_other else core
+    part = chips // PIECES
+    copies = []
+    for n in range(PIECES):
+        tiles = context_ref[n * part : (n + 1) * part].astype(F32).reshape(part, half, 3, feats, LANES)
+        high = tiles[:, :, 2, :, of_other * split : (of_other + 1) * split]
+        context = jnp.concatenate([tiles[:, :, of_other], high], axis=-1).reshape(-1, width)
+        base = base_ref[n * part * half : (n + 1) * part * half].astype(F32).reshape(-1, width)
+        mid = base + jnp.dot(context.astype(BF16), w_out_ref[...], preferred_element_type=F32)
         normed = normed_by(mid, gain_ref[...]).astype(BF16)
         up = jnp.dot(normed, w_up_ref[...], preferred_element_type=F32)
         act = (0.5 * up * (1.0 + lax.erf(up * 0.5**0.5))).astype(BF16)
         out = mid + lax.dot_general(act, w_down_ref[...], NT, preferred_element_type=F32)
-        out = out.reshape(chips, half, feats, width)
-        of_core = core if j == 0 else 1 - core
-        for c in range(chips):
-            out_ref[pl.ds(c * 2 * half + of_core * half, half)] = out[c]
+        at = pl.ds(n * part, part)
+        held_ref[n * part : (n + 1) * part] = out.reshape(part, half, feats, width)
+        copies.append(pltpu.make_async_copy(held_ref.at[at], out_hbm.at[at, of_core], sems.at[n]))
+        copies[-1].start()
+    for copy in copies:
+        copy.wait()
 
 
 def vmem(count):
@@ -175,13 +204,23 @@
     swap = [(0, 1), (1, 0)]
     halves = jax.ShapeDtypeStruct((all_rows // 2, feats, width), BF16)
     packed = jax.ShapeDtypeStruct((chips, all_rows * feats * width // (chips * LANES), LANES), BF16)
+    hbm = pl.BlockSpec(memory_space=pltpu.HBM)
     own, other = pl.pallas_call(
         functools.partial(tokens_kernel, chips),
         out_shape=[halves] * 2,
-        in_specs=[*vmem(4), pl.BlockSpec(memory_space=pltpu.SMEM)],
+        in_specs=[hbm] * 5,
         out_specs=vmem(2),
+        scratch_shapes=[
+            pltpu.VMEM(cells.shape, cells.dtype),
+            pltpu.VMEM(missing.shape[::-1], missing.dtype),
+            pltpu.VMEM(feat_table.shape, F32),
+            pltpu.VMEM((1, width), F32),
+            pltpu.SMEM(feat_ids.shape, feat_ids.dtype),
+            pltpu.SemaphoreType.DMA((4 + PIECES,)),
+        ],
+        compiler_params=limit(12),
         name="tokens",
-    )(cells, missing.T, feat_table, nan_embed[None], feat_ids)
+    )(*(pltpu.with_memory_space_constraint(x, pltpu.HBM) for x in (cells, missing.T, feat_table, nan_embed[None], feat_ids)))
     tokens = pl.pallas_call(
         merge_kernel,
         out_shape=packed,
@@ -194,32 +233,33 @@
     context = pl.pallas_call(
         functools.partial(attention_kernel, feats),
         out_shape=packed,
-        in_specs=vmem(4),
+        in_specs=vmem(3),
         out_specs=vmem(1)[0],
         compiler_params=limit(24),
         name="attend",
-    )(tokens, gain_one[None], w_qkv[:, : 2 * width], w_qkv[:, 2 * width :].T)
+    )(tokens, gain_one[None], w_qkv)
     context = lax.all_to_all(context, "chip", 0, 0, tiled=True)
-    steps = 4 if chips % 4 == 0 else 1
-    some = pl.BlockSpec((chips // steps, *packed.shape[1:]), lambda n: (n, 0, 0))
-    base = pl.BlockSpec((all_rows // 2 // steps, feats, width), lambda n: (n, 0, 0))
-    whole = lambda shape: pl.BlockSpec(shape, lambda n: (0, 0))
-    return pl.pallas_call(
-        functools.partial(finish_kernel, feats),
-        out_shape=jax.ShapeDtypeStruct(cells.shape, F32),
-        grid=(steps,),
-        in_specs=[
-            *[base] * 2,
-            *[some] * 2,
-            whole(w_out.shape),
-            whole((1, width)),
-            whole(w_up.shape),
-            whole(w_down.shape[::-1]),
-        ],
-        out_specs=pl.BlockSpec((all_rows // steps, feats, width), lambda n: (n, 0, 0)),
-        compiler_params=limit(16),
-        name="finish",
-    )(own, other, context, lax.ppermute(context, "core", swap), w_out, gain_two[None], w_up, w_down.T)
+    swapped = lax.ppermute(context, "core", swap)
+    half = all_rows // chips // 2
+    result = jax.ShapeDtypeStruct((chips, 2, half, feats, width), F32)
+
+    def finish(of_other, base, context, *before):
+        return pl.pallas_call(
+            functools.partial(finish_kernel, feats, of_other),
+            out_shape=result,
+            in_specs=[*vmem(6), *[hbm] * len(before)],
+            out_specs=hbm,
+            scratch_shapes=[
+                pltpu.VMEM((chips, half, feats, width), F32),
+                pltpu.SemaphoreType.DMA((PIECES,)),
+            ],
+            input_output_aliases={6: 0} if before else {},
+            compiler_params=limit(16),
+            cost_estimate=pl.CostEstimate(flops=10**9, bytes_accessed=2 * 10**6, transcendentals=0),
+            name="finish",
+        )(base, context, w_out, gain_two[None], w_up, w_down.T, *before)
+
+    return finish(1, other, swapped, finish(0, own, context)).reshape(cells.shape)
 
 
 def solution(mesh):

time: 178 us -> 173 us (0.972)
  blocking collectives: 50.4 us -> 107 us
  waiting for transfers between devices: 47.3 us -> 1.35 us
  starting transfers between devices: 33.8 us -> 20.5 us
    all_to_all x0 -> x1, blocking collectives: none -> 56.4 us  [body(): tokens = lax.all_to_all(tokens, 'chip', 0, 0, tiled=True)]
    all_to_all x1 -> x0, waiting for transfers between devices: 43.7 us -> none  [body(): tokens = lax.all_to_all(tokens, 'chip', 0, 0, tiled=True)]
    all_to_all x1 -> x0, starting transfers between devices: 13.4 us -> none  [body(): tokens = lax.all_to_all(tokens, 'chip', 0, 0, tiled=True)]
    ppermute x1, waiting for transfers between devices: 2 us -> 0.01 us  [body(): swapped = lax.ppermute(context, 'core', swap)]
    pallas_call x1 -> x2, Pallas kernels: 5.41 us -> 5.38 us  [finish(): pl.pallas_call(functools.partial(finish_kernel, feats, of_other), out_sha...]
  transfers between devices with their start and end apart: 3 -> 2, of which waited for: 3 -> 1; matrix products, arithmetic and copies ran while one was open for 0% -> 0% of each run, Pallas kernels for 0% -> 2%
where the time goes in v3:
time: 173 us
  blocking collectives  107 us (62%)
  Pallas kernels  44 us (25%)
  starting transfers between devices  20.5 us (12%)
    all_to_all x1, blocking collectives, body(): tokens = lax.all_to_all(tokens, 'chip', 0, 0, tiled=True)  56.4 us
    all_to_all x1, blocking collectives, body(): context = lax.all_to_all(context, 'chip', 0, 0, tiled=True)  50.2 us
    pallas_call x1, Pallas kernels, body(): pl.pallas_call(merge_kernel, out_shape=packed, in_specs=vmem(2), out_spec...  28.1 us
    ppermute x1, starting transfers between devices, body(): lax.ppermute(other, 'core', swap)  20.5 us
    pallas_call x1, Pallas kernels, body(): pl.pallas_call(functools.partial(attention_kernel, feats), out_shape=pack...  8.82 us
    pallas_call x2, Pallas kernels, finish(): pl.pallas_call(functools.partial(finish_kernel, feats, of_other), out_sha...  5.38 us
  transfers between devices with their start and end apart: 2, of which 1 were waited for; matrix products, arithmetic and copies ran while one was open for 0% of the time, Pallas kernels for 2%

profile of v3, /device:TPU:37, one launch (start us, length us, event | category | flops | bytes accessed | tf_op | source)
XLA Modules:
  0.0 172.6 jit_solution(10337399160706596363)
XLA Ops:
  0.0 0.0 copy-start.2
  0.0 0.0 copy-start.4
  0.0 1.7 tokens.1
  1.7 20.5 %collective-permute-start = (bf16[96,8,192]{2,1,0:T(8,128)(2,1)S(1)}, bf16[96,8,192]{2,1,0:T(8,128)(2,1)S(1)}, u32[]{:S(2)}, u32[]{:S(2)}) collective-permute-start(bf16[96,8,192]{2,1,0:T(8,128)(2,1)S(1)} %get-tuple-element.7.base_ref), channel_id=1, source_target_pairs={{0,1},{1,0},{2,3},{3,2},{4,5},{5,4},{6,7},{7,6},{8,9},{9,8},{10,11... | collective-permute-start | bytes 884744 | tf_op jit(solution)/shard_map/ppermute | solution.py:231
  22.2 1.3 collective-permute-done.other_ref
  23.6 28.1 %merge.1 = bf16[32,72,128]{2,1,0:T(8,128)(2,1)S(1)} custom-call(bf16[96,8,192]{2,1,0:T(8,128)(2,1)S(1)} %get-tuple-element.8.own_ref.base_ref, bf16[96,8,192]{2,1,0:T(8,128)(2,1)S(1)} %collective-permute-done.other_ref), custom_call_target="tpu_custom_call" | custom-call | tf_op jit(solution)/shard_map/merge/pallas_call | solution.py:224
  51.7 56.4 %all_to_all.10.in_ref = bf16[32,72,128]{2,1,0:T(8,128)(2,1)S(1)} all-to-all(bf16[32,72,128]{2,1,0:T(8,128)(2,1)S(1)} %merge.1), channel_id=1, replica_groups=mesh['groups'=4,'chip'=32,'core'=2] {'chip'}, dimensions={0} | all-to-all | bytes 1179648 | tf_op jit(solution)/shard_map/all_to_all | solution.py:232
  108.1 0.0 copy-start
  108.1 0.0 copy-start.1
  108.1 0.0 copy-start.3
  108.2 0.0 copy-start.5
  108.2 0.0 copy-done.2
  108.2 0.0 copy-done.4
  108.2 8.8 %attend.1 = bf16[32,72,128]{2,1,0:T(8,128)(2,1)S(1)} custom-call(bf16[32,72,128]{2,1,0:T(8,128)(2,1)S(1)} %all_to_all.10.in_ref, f32[1,192]{1,0:T(1,128)S(1)} %bitcast.8, bf16[192,576]{1,0:T(8,128)(2,1)S(1)} %copy-done.2), custom_call_target="tpu_custom_call" | custom-call | tf_op jit(solution)/shard_map/attend/pallas_call | solution.py:233
  117.0 50.2 %all_to_all.11.context_ref = bf16[32,72,128]{2,1,0:T(8,128)(2,1)S(1)} all-to-all(bf16[32,72,128]{2,1,0:T(8,128)(2,1)S(1)} %attend.1), channel_id=1, replica_groups=mesh['groups'=4,'chip'=32,'core'=2] {'chip'}, dimensions={0} | all-to-all | bytes 1179648 | tf_op jit(solution)/shard_map/all_to_all | solution.py:241
  167.2 0.0 collective-permute-start.1
  167.2 0.0 copy-done
  167.2 0.0 copy-done.1
  167.2 0.0 copy-done.3
  167.2 0.0 copy-done.5
  167.2 2.7 %finish.2.rest_0_ = f32[32,2,3,8,192]{4,3,2,1,0:T(8,128)} custom-call(bf16[96,8,192]{2,1,0:T(8,128)(2,1)S(1)} %get-tuple-element.8.own_ref.base_ref, bf16[32,72,128]{2,1,0:T(8,128)(2,1)S(1)} %all_to_all.11.context_ref, bf16[192,192]{1,0:T(8,128)(2,1)S(1)} %copy-done.3, f32[1,192]{1,0:T(1,128)S(1)} %bitcast.9, bf16[192,768]{1,0:T(8,128)(2,1)S(1)} %copy-done, ...), custom_call_target="tpu_custom_call" | custom-call | flops 1000000000 | bytes 2000000 | tf_op jit(solution)/shard_map/finish/pallas_call | solution.py:247
  169.9 0.0 collective-permute-done.1.context_ref
  169.9 2.7 %finish.3 = f32[32,2,3,8,192]{4,3,2,1,0:T(8,128)} custom-call(bf16[96,8,192]{2,1,0:T(8,128)(2,1)S(1)} %get-tuple-element.7.base_ref, bf16[32,72,128]{2,1,0:T(8,128)(2,1)S(1)} %collective-permute-done.1.context_ref, bf16[192,192]{1,0:T(8,128)(2,1)S(1)} %copy-done.3, f32[1,192]{1,0:T(1,128)S(1)} %bitcast.10, ...), custom_call_target="tpu_custom_call", output_to_operand_aliasing={{}: (6, {})} | custom-call | flops 1000000000 | bytes 2000000 | tf_op jit(solution)/shard_map/finish/pallas_call | solution.py:247
Async XLA Ops:
  0.0 108.2 %copy-start.2 = (bf16[192,576]{1,0:T(8,128)(2,1)S(1)}, bf16[192,576]{1,0:T(8,128)(2,1)}, u32[]{:S(2)}) copy-start(bf16[192,576]{1,0:T(8,128)(2,1)} %w_ref.1) | copy-start | bytes 663556
  0.0 108.2 %copy-start.4 = (f32[192]{0:T(256)S(1)}, f32[192]{0:T(256)}, u32[]{:S(2)}) copy-start(f32[192]{0:T(256)} %param.16) | copy-start | bytes 2308
  1.7 21.9 %collective-permute-start = (bf16[96,8,192]{2,1,0:T(8,128)(2,1)S(1)}, bf16[96,8,192]{2,1,0:T(8,128)(2,1)S(1)}, u32[]{:S(2)}, u32[]{:S(2)}) collective-permute-start(bf16[96,8,192]{2,1,0:T(8,128)(2,1)S(1)} %get-tuple-element.7.base_ref), channel_id=1, source_target_pairs={{0,1},{1,0},{2,3},{3,2},{4,5},{5,4},{6,7},{7,6},{8,9},{9,8},{10,11... | collective-permute-start | bytes 884744 | tf_op jit(solution)/shard_map/ppermute | solution.py:231
  108.1 59.0 %copy-start = (bf16[192,768]{1,0:T(8,128)(2,1)S(1)}, bf16[192,768]{1,0:T(8,128)(2,1)}, u32[]{:S(2)}) copy-start(bf16[192,768]{1,0:T(8,128)(2,1)} %w_up_ref.3) | copy-start | bytes 884740
  108.1 59.0 %copy-start.1 = (bf16[768,192]{0,1:T(8,128)(2,1)S(1)}, bf16[768,192]{0,1:T(8,128)(2,1)}, u32[]{:S(2)}) copy-start(bf16[768,192]{0,1:T(8,128)(2,1)} %param.21) | copy-start | bytes 884740
  108.1 59.0 %copy-start.3 = (bf16[192,192]{1,0:T(8,128)(2,1)S(1)}, bf16[192,192]{1,0:T(8,128)(2,1)}, u32[]{:S(2)}) copy-start(bf16[192,192]{1,0:T(8,128)(2,1)} %w_out_ref.3) | copy-start | bytes 221188
  108.2 59.1 %copy-start.5 = (f32[192]{0:T(256)S(1)}, f32[192]{0:T(256)}, u32[]{:S(2)}) copy-start(f32[192]{0:T(256)} %param.19) | copy-start | bytes 2308
  167.2 2.7 %collective-permute-start.1 = (bf16[32,72,128]{2,1,0:T(8,128)(2,1)S(1)}, bf16[32,72,128]{2,1,0:T(8,128)(2,1)S(1)}, u32[]{:S(2)}, u32[]{:S(2)}) collective-permute-start(bf16[32,72,128]{2,1,0:T(8,128)(2,1)S(1)} %all_to_all.11.context_ref), channel_id=1, source_target_pairs={{0,1},{1,0},{2,3},{3,2},{4,5},{5,4},{6,7},{7,6},{8,9},{9,8},{10,11... | collective-permute-start | bytes 1769480 | tf_op jit(solution)/shard_map/ppermute | solution.py:242

commit v4 on v3

--- a/solution.py
+++ b/solution.py
@@ -11,8 +11,9 @@
 HEADS = 6
 LANES = 128
 ONES = 16
-LEAD, LAG = 2, 1
-HOLD_NS = 28000
+LEAD, LAG = 2,1
+EARLY = 1
+HOLD_NS = 27000
 PIECES = 4
 FEAT = ("chip", "core")
 ALL = ("groups", "chip", "core")
@@ -119,8 +120,7 @@
         part = jnp.dot(mine, expo, preferred_element_type=F32)
         return part[:head_dim] * (1.0 / part[head_dim : head_dim + 1])
 
-    @pl.loop(0, in_ref.shape[1] // (3 * feats))
-    def _(i):
+    def ready(i):
         high = flat(i, 2)
         values = jnp.concatenate(
             [
@@ -133,57 +133,88 @@
         q = jnp.dot(normed, w_ref[:, :width], preferred_element_type=F32).astype(BF16)
         k = jnp.dot(normed, w_ref[:, width : 2 * width], preferred_element_type=F32).astype(BF16)
         v = lax.dot_general(w_ref[:, 2 * width :], normed, TT, preferred_element_type=F32).astype(BF16)
-        sides = [q[:cells], q[cells:]]
-        pairs = [(h, side) for h in range(HEADS) for side in range(2)]
-        ahead = [scores_of(sides[side], k, h) for h, side in pairs[:LEAD]]
-        done = [[], []]
-        expos = []
-        for n, (h, side) in enumerate(pairs):
-            if n + LEAD < len(pairs):
-                h2, side2 = pairs[n + LEAD]
-                ahead.append(scores_of(sides[side2], k, h2))
-            expos.append(softmax(ahead.pop(0)))
-            if n >= LAG:
-                h0, side0 = pairs[n - LAG]
-                done[side0].append(context_of(v, expos.pop(0), h0))
-        for h0, side0 in pairs[len(pairs) - LAG :]:
-            done[side0].append(context_of(v, expos.pop(0), h0))
+        return (q[:cells], q[cells:]), k, v
+
+    def put(i, done):
         highs = []
         for side in range(2):
-            done[side].append(jnp.zeros((2 * LANES - width, cells), F32))
-            context = jnp.concatenate(done[side], axis=0).T
+            rest = jnp.zeros((2 * LANES - width, cells), F32)
+            context = jnp.concatenate([*done[side], rest], axis=0).T
             out_ref[:, tile(i, side), :] = context[:, :LANES].reshape(chips, feats, LANES).astype(BF16)
             highs.append(context[:, LANES:width])
         high = jnp.concatenate(highs, axis=1).reshape(chips, feats, LANES)
         out_ref[:, tile(i, 2), :] = high.astype(BF16)
 
+    count = in_ref.shape[1] // (3 * feats)
+    units = [(i, h, side) for i in range(count) for h in range(HEADS) for side in range(2)]
+    made = {0: ready(0)}
+    done = {(i, side): [] for i in range(count) for side in range(2)}
+    ahead, expos = [], []
+
+    def issue(n):
+        i, h, side = units[n]
+        ahead.append(scores_of(made[i][0][side], made[i][1], h))
+
+    def retire(n):
+        i, h, side = units[n]
+        done[i, side].append(context_of(made[i][2], expos.pop(0), h))
+        if (h, side) == (HEADS - 1, 1):
+            put(i, [done[i, 0], done[i, 1]])
+
+    for n in range(LEAD):
+        issue(n)
+    for n, (i, h, side) in enumerate(units):
+        if (h, side) == (EARLY, 0) and i + 1 < count:
+            made[i + 1] = ready(i + 1)
+        if n + LEAD < len(units):
+            issue(n + LEAD)
+        expos.append(softmax(ahead.pop(0)))
+        if n >= LAG:
+            retire(n - LAG)
+    for n in range(len(units) - LAG, len(units)):
+        retire(n)
+
 
 def finish_kernel(
     feats, of_other, base_ref, context_ref, w_out_ref, gain_ref, w_up_ref, w_down_ref, *rest
 ):
-    out_hbm, held_ref, sems = rest[-3:]
     width = gain_ref.shape[-1]
     chips = context_ref.shape[0]
     half = context_ref.shape[1] // (3 * feats)
     split = LANES // 2
     core = lax.axis_index("core")
-    of_core = 1 - core if of_other else core
-    part = chips // PIECES
+    pieces = PIECES if of_other else 2
+    part = chips // pieces
     copies = []
-    for n in range(PIECES):
+
+    def copy_out(source, n, of_core):
+        at = pl.ds(n * part, part)
+        copies.append(pltpu.make_async_copy(source.at[at], out_hbm.at[at, of_core], sems.at[len(copies)]))
+        copies[-1].start()
+
+    if of_other:
+        first_ref, out_hbm, held_ref, sems = rest
+        for n in range(pieces):
+            copy_out(first_ref, n, core)
+    else:
+        (held_ref,) = rest
+
+    def start(n):
         tiles = context_ref[n * part : (n + 1) * part].astype(F32).reshape(part, half, 3, feats, LANES)
         high = tiles[:, :, 2, :, of_other * split : (of_other + 1) * split]
         context = jnp.concatenate([tiles[:, :, of_other], high], axis=-1).reshape(-1, width)
         base = base_ref[n * part * half : (n + 1) * part * half].astype(F32).reshape(-1, width)
         mid = base + jnp.dot(context.astype(BF16), w_out_ref[...], preferred_element_type=F32)
         normed = normed_by(mid, gain_ref[...]).astype(BF16)
-        up = jnp.dot(normed, w_up_ref[...], preferred_element_type=F32)
+        return mid, jnp.dot(normed, w_up_ref[...], preferred_element_type=F32)
+
+    for n in range(pieces):
+        mid, up = start(n)
         act = (0.5 * up * (1.0 + lax.erf(up * 0.5**0.5))).astype(BF16)
         out = mid + lax.dot_general(act, w_down_ref[...], NT, preferred_element_type=F32)
-        at = pl.ds(n * part, part)
         held_ref[n * part : (n + 1) * part] = out.reshape(part, half, feats, width)
-        copies.append(pltpu.make_async_copy(held_ref.at[at], out_hbm.at[at, of_core], sems.at[n]))
-        copies[-1].start()
+        if of_other:
+            copy_out(held_ref, n, 1 - core)
     for copy in copies:
         copy.wait()
 
@@ -241,19 +272,17 @@
     context = lax.all_to_all(context, "chip", 0, 0, tiled=True)
     swapped = lax.ppermute(context, "core", swap)
     half = all_rows // chips // 2
-    result = jax.ShapeDtypeStruct((chips, 2, half, feats, width), F32)
+    both = jax.ShapeDtypeStruct((chips, 2, half, feats, width), F32)
+    one = jax.ShapeDtypeStruct((chips, half, feats, width), F32)
 
     def finish(of_other, base, context, *before):
+        scratch = [pltpu.VMEM(one.shape, F32), pltpu.SemaphoreType.DMA((2 * PIECES,))]
         return pl.pallas_call(
             functools.partial(finish_kernel, feats, of_other),
-            out_shape=result,
-            in_specs=[*vmem(6), *[hbm] * len(before)],
-            out_specs=hbm,
-            scratch_shapes=[
-                pltpu.VMEM((chips, half, feats, width), F32),
-                pltpu.SemaphoreType.DMA((PIECES,)),
-            ],
-            input_output_aliases={6: 0} if before else {},
+            out_shape=both if of_other else one,
+            in_specs=vmem(6 + len(before)),
+            out_specs=hbm if of_other else vmem(1)[0],
+            scratch_shapes=scratch if of_other else [],
             compiler_params=limit(16),
             cost_estimate=pl.CostEstimate(flops=10**9, bytes_accessed=2 * 10**6, transcendentals=0),
             name="finish",

time: 173 us -> 170 us (0.983)
  Pallas kernels: 44 us -> 40 us
    pallas_call x1, Pallas kernels: 8.82 us -> 6.86 us  [body(): pl.pallas_call(functools.partial(attention_kernel, feats), out_shape=pack...]
  transfers between devices with their start and end apart: 2 -> 2, of which waited for: 1 -> 2; matrix products, arithmetic and copies ran while one was open for 0% -> 0% of each run, Pallas kernels for 2% -> 1%
where the time goes in v4:
time: 170 us
  blocking collectives  108 us (64%)
  Pallas kernels  40 us (24%)
  starting transfers between devices  20.5 us (12%)
  waiting for transfers between devices  1.74 us (1%)
    all_to_all x1, blocking collectives, body(): tokens = lax.all_to_all(tokens, 'chip', 0, 0, tiled=True)  57.1 us
    all_to_all x1, blocking collectives, body(): context = lax.all_to_all(context, 'chip', 0, 0, tiled=True)  50.5 us
    pallas_call x1, Pallas kernels, body(): pl.pallas_call(merge_kernel, out_shape=packed, in_specs=vmem(2), out_spec...  27.1 us
    ppermute x1, starting transfers between devices, body(): lax.ppermute(other, 'core', swap)  20.5 us
    pallas_call x1, Pallas kernels, body(): pl.pallas_call(functools.partial(attention_kernel, feats), out_shape=pack...  6.86 us
    pallas_call x2, Pallas kernels, finish(): pl.pallas_call(functools.partial(finish_kernel, feats, of_other), out_sha...  4.29 us
  transfers between devices with their start and end apart: 2, of which 2 were waited for; matrix products, arithmetic and copies ran while one was open for 0% of the time, Pallas kernels for 1%

profile of v4, /device:TPU:37, one launch (start us, length us, event | category | flops | bytes accessed | tf_op | source)
XLA Modules:
  0.0 170.0 jit_solution(7609293883293858085)
XLA Ops:
  0.0 0.0 copy-start.2
  0.0 0.0 copy-start.4
  0.0 1.7 tokens.1
  1.7 20.5 %collective-permute-start = (bf16[96,8,192]{2,1,0:T(8,128)(2,1)S(1)}, bf16[96,8,192]{2,1,0:T(8,128)(2,1)S(1)}, u32[]{:S(2)}, u32[]{:S(2)}) collective-permute-start(bf16[96,8,192]{2,1,0:T(8,128)(2,1)S(1)} %get-tuple-element.7.base_ref), channel_id=1, source_target_pairs={{0,1},{1,0},{2,3},{3,2},{4,5},{5,4},{6,7},{7,6},{8,9},{9,8},{10,11... | collective-permute-start | bytes 884744 | tf_op jit(solution)/shard_map/ppermute | solution.py:262
  22.2 1.3 collective-permute-done.other_ref
  23.6 27.1 %merge.1 = bf16[32,72,128]{2,1,0:T(8,128)(2,1)S(1)} custom-call(bf16[96,8,192]{2,1,0:T(8,128)(2,1)S(1)} %get-tuple-element.8.own_ref.base_ref, bf16[96,8,192]{2,1,0:T(8,128)(2,1)S(1)} %collective-permute-done.other_ref), custom_call_target="tpu_custom_call" | custom-call | tf_op jit(solution)/shard_map/merge/pallas_call | solution.py:255
  50.7 57.1 %all_to_all.10.in_ref = bf16[32,72,128]{2,1,0:T(8,128)(2,1)S(1)} all-to-all(bf16[32,72,128]{2,1,0:T(8,128)(2,1)S(1)} %merge.1), channel_id=1, replica_groups=mesh['groups'=4,'chip'=32,'core'=2] {'chip'}, dimensions={0} | all-to-all | bytes 1179648 | tf_op jit(solution)/shard_map/all_to_all | solution.py:263
  107.8 0.0 copy-start
  107.8 0.0 copy-start.1
  107.8 0.0 copy-start.3
  107.8 0.0 copy-start.5
  107.8 0.0 copy-done.2
  107.8 0.0 copy-done.4
  107.8 6.9 %attend.1 = bf16[32,72,128]{2,1,0:T(8,128)(2,1)S(1)} custom-call(bf16[32,72,128]{2,1,0:T(8,128)(2,1)S(1)} %all_to_all.10.in_ref, f32[1,192]{1,0:T(1,128)S(1)} %bitcast.8, bf16[192,576]{1,0:T(8,128)(2,1)S(1)} %copy-done.2), custom_call_target="tpu_custom_call" | custom-call | tf_op jit(solution)/shard_map/attend/pallas_call | solution.py:264
  114.7 50.5 %all_to_all.11.context_ref = bf16[32,72,128]{2,1,0:T(8,128)(2,1)S(1)} all-to-all(bf16[32,72,128]{2,1,0:T(8,128)(2,1)S(1)} %attend.1), channel_id=1, replica_groups=mesh['groups'=4,'chip'=32,'core'=2] {'chip'}, dimensions={0} | all-to-all | bytes 1179648 | tf_op jit(solution)/shard_map/all_to_all | solution.py:272
  165.2 0.0 collective-permute-start.1
  165.2 0.0 copy-done
  165.2 0.0 copy-done.1
  165.2 0.0 copy-done.3
  165.2 0.0 copy-done.5
  165.2 1.6 finish.2.rest_0_
  166.8 0.4 collective-permute-done.1.context_ref
  167.2 2.7 %finish.3 = f32[32,2,3,8,192]{4,3,2,1,0:T(8,128)} custom-call(bf16[96,8,192]{2,1,0:T(8,128)(2,1)S(1)} %get-tuple-element.7.base_ref, bf16[32,72,128]{2,1,0:T(8,128)(2,1)S(1)} %collective-permute-done.1.context_ref, bf16[192,192]{1,0:T(8,128)(2,1)S(1)} %copy-done.3, f32[1,192]{1,0:T(1,128)S(1)} %bitcast.10, bf16[192,768]{1,0:T(8,128)(2,1)S(1)} %copy-done, ...), custom_call_target="tpu_custom_call" | custom-call | flops 1000000000 | bytes 2000000 | tf_op jit(solution)/shard_map/finish/pallas_call | solution.py:280
Async XLA Ops:
  0.0 107.8 %copy-start.2 = (bf16[192,576]{1,0:T(8,128)(2,1)S(1)}, bf16[192,576]{1,0:T(8,128)(2,1)}, u32[]{:S(2)}) copy-start(bf16[192,576]{1,0:T(8,128)(2,1)} %w_ref.1) | copy-start | bytes 663556
  0.0 107.8 %copy-start.4 = (f32[192]{0:T(256)S(1)}, f32[192]{0:T(256)}, u32[]{:S(2)}) copy-start(f32[192]{0:T(256)} %param.16) | copy-start | bytes 2308
  1.7 21.9 %collective-permute-start = (bf16[96,8,192]{2,1,0:T(8,128)(2,1)S(1)}, bf16[96,8,192]{2,1,0:T(8,128)(2,1)S(1)}, u32[]{:S(2)}, u32[]{:S(2)}) collective-permute-start(bf16[96,8,192]{2,1,0:T(8,128)(2,1)S(1)} %get-tuple-element.7.base_ref), channel_id=1, source_target_pairs={{0,1},{1,0},{2,3},{3,2},{4,5},{5,4},{6,7},{7,6},{8,9},{9,8},{10,11... | collective-permute-start | bytes 884744 | tf_op jit(solution)/shard_map/ppermute | solution.py:262
  107.8 57.4 %copy-start = (bf16[192,768]{1,0:T(8,128)(2,1)S(1)}, bf16[192,768]{1,0:T(8,128)(2,1)}, u32[]{:S(2)}) copy-start(bf16[192,768]{1,0:T(8,128)(2,1)} %w_up_ref.3) | copy-start | bytes 884740
  107.8 57.4 %copy-start.1 = (bf16[768,192]{0,1:T(8,128)(2,1)S(1)}, bf16[768,192]{0,1:T(8,128)(2,1)}, u32[]{:S(2)}) copy-start(bf16[768,192]{0,1:T(8,128)(2,1)} %param.21) | copy-start | bytes 884740
  107.8 57.4 %copy-start.3 = (bf16[192,192]{1,0:T(8,128)(2,1)S(1)}, bf16[192,192]{1,0:T(8,128)(2,1)}, u32[]{:S(2)}) copy-start(bf16[192,192]{1,0:T(8,128)(2,1)} %w_out_ref.3) | copy-start | bytes 221188
  107.8 57.4 %copy-start.5 = (f32[192]{0:T(256)S(1)}, f32[192]{0:T(256)}, u32[]{:S(2)}) copy-start(f32[192]{0:T(256)} %param.19) | copy-start | bytes 2308
  165.2 2.0 %collective-permute-start.1 = (bf16[32,72,128]{2,1,0:T(8,128)(2,1)S(1)}, bf16[32,72,128]{2,1,0:T(8,128)(2,1)S(1)}, u32[]{:S(2)}, u32[]{:S(2)}) collective-permute-start(bf16[32,72,128]{2,1,0:T(8,128)(2,1)S(1)} %all_to_all.11.context_ref), channel_id=1, source_target_pairs={{0,1},{1,0},{2,3},{3,2},{4,5},{5,4},{6,7},{7,6},{8,9},{9,8},{10,11... | collective-permute-start | bytes 1769480 | tf_op jit(solution)/shard_map/ppermute | solution.py:273

commit v5 on v4

--- a/solution.py
+++ b/solution.py
@@ -183,7 +183,7 @@
     half = context_ref.shape[1] // (3 * feats)
     split = LANES // 2
     core = lax.axis_index("core")
-    pieces = PIECES if of_other else 2
+    pieces = 2
     part = chips // pieces
     copies = []
 
@@ -194,8 +194,8 @@
 
     if of_other:
         first_ref, out_hbm, held_ref, sems = rest
-        for n in range(pieces):
-            copy_out(first_ref, n, core)
+        copies.append(pltpu.make_async_copy(first_ref, out_hbm.at[:, core], sems.at[0]))
+        copies[0].start()
     else:
         (held_ref,) = rest
 

time: 170 us -> 170 us (level)
  no operation moved by 1% of the time
where the time goes in v5:
time: 170 us
  blocking collectives  108 us (64%)
  Pallas kernels  39.8 us (23%)
  starting transfers between devices  20.5 us (12%)
  waiting for transfers between devices  1.74 us (1%)
    all_to_all x1, blocking collectives, body(): tokens = lax.all_to_all(tokens, 'chip', 0, 0, tiled=True)  57.1 us
    all_to_all x1, blocking collectives, body(): context = lax.all_to_all(context, 'chip', 0, 0, tiled=True)  50.5 us
    pallas_call x1, Pallas kernels, body(): pl.pallas_call(merge_kernel, out_shape=packed, in_specs=vmem(2), out_spec...  27.1 us
    ppermute x1, starting transfers between devices, body(): lax.ppermute(other, 'core', swap)  20.5 us
    pallas_call x1, Pallas kernels, body(): pl.pallas_call(functools.partial(attention_kernel, feats), out_shape=pack...  6.86 us
    pallas_call x2, Pallas kernels, finish(): pl.pallas_call(functools.partial(finish_kernel, feats, of_other), out_sha...  4.11 us
  transfers between devices with their start and end apart: 2, of which 2 were waited for; matrix products, arithmetic and copies ran while one was open for 0% of the time, Pallas kernels for 1%

profile of v5, /device:TPU:37, one launch (start us, length us, event | category | flops | bytes accessed | tf_op | source)
XLA Modules:
  0.0 169.9 jit_solution(15882455545651162825)
XLA Ops:
  0.0 0.0 copy-start.2
  0.0 0.0 copy-start.4
  0.0 1.7 tokens.1
  1.7 20.5 %collective-permute-start = (bf16[96,8,192]{2,1,0:T(8,128)(2,1)S(1)}, bf16[96,8,192]{2,1,0:T(8,128)(2,1)S(1)}, u32[]{:S(2)}, u32[]{:S(2)}) collective-permute-start(bf16[96,8,192]{2,1,0:T(8,128)(2,1)S(1)} %get-tuple-element.7.base_ref), channel_id=1, source_target_pairs={{0,1},{1,0},{2,3},{3,2},{4,5},{5,4},{6,7},{7,6},{8,9},{9,8},{10,11... | collective-permute-start | bytes 884744 | tf_op jit(solution)/shard_map/ppermute | solution.py:262
  22.2 1.3 collective-permute-done.other_ref
  23.6 27.1 %merge.1 = bf16[32,72,128]{2,1,0:T(8,128)(2,1)S(1)} custom-call(bf16[96,8,192]{2,1,0:T(8,128)(2,1)S(1)} %get-tuple-element.8.own_ref.base_ref, bf16[96,8,192]{2,1,0:T(8,128)(2,1)S(1)} %collective-permute-done.other_ref), custom_call_target="tpu_custom_call" | custom-call | tf_op jit(solution)/shard_map/merge/pallas_call | solution.py:255
  50.7 57.1 %all_to_all.10.in_ref = bf16[32,72,128]{2,1,0:T(8,128)(2,1)S(1)} all-to-all(bf16[32,72,128]{2,1,0:T(8,128)(2,1)S(1)} %merge.1), channel_id=1, replica_groups=mesh['groups'=4,'chip'=32,'core'=2] {'chip'}, dimensions={0} | all-to-all | bytes 1179648 | tf_op jit(solution)/shard_map/all_to_all | solution.py:263
  107.8 0.0 copy-start
  107.8 0.0 copy-start.1
  107.8 0.0 copy-start.3
  107.8 0.0 copy-start.5
  107.8 0.0 copy-done.2
  107.8 0.0 copy-done.4
  107.8 6.9 %attend.1 = bf16[32,72,128]{2,1,0:T(8,128)(2,1)S(1)} custom-call(bf16[32,72,128]{2,1,0:T(8,128)(2,1)S(1)} %all_to_all.10.in_ref, f32[1,192]{1,0:T(1,128)S(1)} %bitcast.8, bf16[192,576]{1,0:T(8,128)(2,1)S(1)} %copy-done.2), custom_call_target="tpu_custom_call" | custom-call | tf_op jit(solution)/shard_map/attend/pallas_call | solution.py:264
  114.7 50.5 %all_to_all.11.context_ref = bf16[32,72,128]{2,1,0:T(8,128)(2,1)S(1)} all-to-all(bf16[32,72,128]{2,1,0:T(8,128)(2,1)S(1)} %attend.1), channel_id=1, replica_groups=mesh['groups'=4,'chip'=32,'core'=2] {'chip'}, dimensions={0} | all-to-all | bytes 1179648 | tf_op jit(solution)/shard_map/all_to_all | solution.py:272
  165.2 0.0 collective-permute-start.1
  165.2 0.0 copy-done
  165.2 0.0 copy-done.1
  165.2 0.0 copy-done.3
  165.2 0.0 copy-done.5
  165.2 1.6 finish.2.rest_0_
  166.8 0.4 collective-permute-done.1.context_ref
  167.2 2.5 %finish.3 = f32[32,2,3,8,192]{4,3,2,1,0:T(8,128)} custom-call(bf16[96,8,192]{2,1,0:T(8,128)(2,1)S(1)} %get-tuple-element.7.base_ref, bf16[32,72,128]{2,1,0:T(8,128)(2,1)S(1)} %collective-permute-done.1.context_ref, bf16[192,192]{1,0:T(8,128)(2,1)S(1)} %copy-done.3, f32[1,192]{1,0:T(1,128)S(1)} %bitcast.10, bf16[192,768]{1,0:T(8,128)(2,1)S(1)} %copy-done, ...), custom_call_target="tpu_custom_call" | custom-call | flops 1000000000 | bytes 2000000 | tf_op jit(solution)/shard_map/finish/pallas_call | solution.py:280
Async XLA Ops:
  0.0 107.8 %copy-start.2 = (bf16[192,576]{1,0:T(8,128)(2,1)S(1)}, bf16[192,576]{1,0:T(8,128)(2,1)}, u32[]{:S(2)}) copy-start(bf16[192,576]{1,0:T(8,128)(2,1)} %w_ref.1) | copy-start | bytes 663556
  0.0 107.8 %copy-start.4 = (f32[192]{0:T(256)S(1)}, f32[192]{0:T(256)}, u32[]{:S(2)}) copy-start(f32[192]{0:T(256)} %param.16) | copy-start | bytes 2308
  1.7 21.9 %collective-permute-start = (bf16[96,8,192]{2,1,0:T(8,128)(2,1)S(1)}, bf16[96,8,192]{2,1,0:T(8,128)(2,1)S(1)}, u32[]{:S(2)}, u32[]{:S(2)}) collective-permute-start(bf16[96,8,192]{2,1,0:T(8,128)(2,1)S(1)} %get-tuple-element.7.base_ref), channel_id=1, source_target_pairs={{0,1},{1,0},{2,3},{3,2},{4,5},{5,4},{6,7},{7,6},{8,9},{9,8},{10,11... | collective-permute-start | bytes 884744 | tf_op jit(solution)/shard_map/ppermute | solution.py:262
  107.8 57.4 %copy-start = (bf16[192,768]{1,0:T(8,128)(2,1)S(1)}, bf16[192,768]{1,0:T(8,128)(2,1)}, u32[]{:S(2)}) copy-start(bf16[192,768]{1,0:T(8,128)(2,1)} %w_up_ref.3) | copy-start | bytes 884740
  107.8 57.4 %copy-start.1 = (bf16[768,192]{0,1:T(8,128)(2,1)S(1)}, bf16[768,192]{0,1:T(8,128)(2,1)}, u32[]{:S(2)}) copy-start(bf16[768,192]{0,1:T(8,128)(2,1)} %param.21) | copy-start | bytes 884740
  107.8 57.4 %copy-start.3 = (bf16[192,192]{1,0:T(8,128)(2,1)S(1)}, bf16[192,192]{1,0:T(8,128)(2,1)}, u32[]{:S(2)}) copy-start(bf16[192,192]{1,0:T(8,128)(2,1)} %w_out_ref.3) | copy-start | bytes 221188
  107.8 57.4 %copy-start.5 = (f32[192]{0:T(256)S(1)}, f32[192]{0:T(256)}, u32[]{:S(2)}) copy-start(f32[192]{0:T(256)} %param.19) | copy-start | bytes 2308
  165.2 2.0 %collective-permute-start.1 = (bf16[32,72,128]{2,1,0:T(8,128)(2,1)S(1)}, bf16[32,72,128]{2,1,0:T(8,128)(2,1)S(1)}, u32[]{:S(2)}, u32[]{:S(2)}) collective-permute-start(bf16[32,72,128]{2,1,0:T(8,128)(2,1)S(1)} %all_to_all.11.context_ref), channel_id=1, source_target_pairs={{0,1},{1,0},{2,3},{3,2},{4,5},{5,4},{6,7},{7,6},{8,9},{9,8},{10,11... | collective-permute-start | bytes 1769480 | tf_op jit(solution)/shard_map/ppermute | solution.py:273
